TPU v7x, 16 devices: a whole 2x2x2 slice. The times are simulated.
16 devices in a mesh: dp: 2 (over z), ep: 8 (over y, x, core).
Axes of the slice: x: 2, y: 2, z: 2, core: 2. Of those that a mesh axis runs over, the one named last changes fastest.
Arguments:
- x_tokens: bfloat16 [131072, 768], P(('dp', 'ep'))
- modality: int32 [131072], P(('dp', 'ep'))
- router: float32 [768, 16], replicated
- expert_ids: int32 [131072], P(('dp', 'ep'))
- priority: int32 [131072], P(('dp', 'ep'))
- w_in: bfloat16 [16, 768, 3072], P('ep')
- b_in: bfloat16 [16, 3072], P('ep')
- w_out: bfloat16 [16, 3072, 768], P('ep')
- b_out: bfloat16 [16, 768], P('ep')
- dy_out: bfloat16 [131072, 768], P(('dp', 'ep'))
Outputs:
- output 1: bfloat16 [131072, 768], P(('dp', 'ep'))
- output 2: float32 [], replicated
- output 3: bfloat16 [131072, 768], P(('dp', 'ep'))
- output 4: float32 [768, 16], replicated
- output 5: bfloat16 [16, 768, 3072], P('ep')
- output 6: bfloat16 [16, 3072], P('ep')
- output 7: bfloat16 [16, 3072, 768], P('ep')
- output 8: bfloat16 [16, 768], P('ep')
All inputs are finite; a program needn't handle non-finite values.
Results may differ from a plain program's by a relative error of at most 0.00946413.
Values are sent between devices in bfloat16 or wider.
A program may use at most 1 GiB of HBM per device.

v0:
```python
import jax
import jax.numpy as jnp
from jax import lax
from jax.sharding import PartitionSpec as P

ALL_AXES = ("dp", "ep")


def route_tokens(expert_ids, priority, num_experts, capacity):
    num_tokens = expert_ids.shape[0]
    sort_order = jnp.argsort(expert_ids * num_tokens + priority)
    sorted_rank = jnp.argsort(sort_order)
    counts = jnp.sum((expert_ids[:, None] == jnp.arange(num_experts)[None, :]).astype(jnp.int32), axis=0)
    starts = jnp.cumsum(counts) - counts
    slot_rank = jnp.arange(capacity)
    slot_token = sort_order[jnp.minimum(starts[:, None] + slot_rank[None, :], num_tokens - 1)]
    slot_valid = slot_rank[None, :] < counts[:, None]
    position = sorted_rank - starts[expert_ids]
    keep_mask = position < capacity
    token_slot = expert_ids * capacity + jnp.minimum(position, capacity - 1)
    return slot_token, slot_valid, token_slot, keep_mask


def router_forward(x_loc, modality, router, expert_ids):
    num_experts = router.shape[1]
    logits = jnp.dot(x_loc, router, precision=lax.Precision.HIGHEST, preferred_element_type=jnp.float32)
    log_probs = jax.nn.log_softmax(logits, axis=-1)
    router_probs = jnp.exp(log_probs)
    expert_onehot = (expert_ids[:, None] == jnp.arange(num_experts)[None, :]).astype(jnp.float32)
    gate_prob = jnp.sum(router_probs * expert_onehot, axis=-1)
    mod_mask = jnp.stack([modality == 0, modality == 1]).astype(jnp.float32)
    entropy = -jnp.sum(router_probs * log_probs, axis=-1)
    local_stats = jnp.concatenate([jnp.dot(mod_mask, router_probs), jnp.dot(mod_mask, entropy)[:, None], jnp.sum(mod_mask, axis=1, keepdims=True)], axis=1)
    return log_probs, router_probs, expert_onehot, gate_prob, mod_mask, local_stats


def aux_from_stats(stats, num_experts):
    mod_count = stats[:, num_experts + 1]
    mean_probs = stats[:, :num_experts] / mod_count[:, None]
    aux_loss = jnp.sum(stats[:, num_experts] / mod_count) + jnp.sum(mean_probs * jnp.log(mean_probs))
    return aux_loss, mean_probs, mod_count


def router_backward(x_loc, router, log_probs, router_probs, expert_onehot, mod_mask, mean_probs, mod_count, d_gate):
    inv_count = jnp.dot(1.0 / mod_count, mod_mask)
    global_part = jnp.einsum("mt,me->te", mod_mask, jnp.log(mean_probs) / mod_count[:, None])
    d_probs = expert_onehot * d_gate[:, None] + global_part - log_probs * inv_count[:, None]
    d_logits = router_probs * (d_probs - jnp.sum(d_probs * router_probs, axis=-1, keepdims=True))
    d_router_part = jnp.einsum("tw,te->we", x_loc, d_logits, precision=lax.Precision.HIGHEST, preferred_element_type=jnp.float32)
    dx_router = jnp.einsum("te,we->tw", d_logits, router, precision=lax.Precision.HIGHEST, preferred_element_type=jnp.float32)
    return d_router_part, dx_router.astype(jnp.bfloat16)


def solution(mesh):
    token_spec = P(ALL_AXES)
    expert_spec = P("ep")

    def local_step(x_loc, modality, router, expert_ids, priority, w_in, b_in, w_out, b_out, dy_loc):
        num_tokens, model_width = x_loc.shape
        num_experts = router.shape[1]
        capacity = num_tokens // num_experts
        slot_token, slot_valid, token_slot, keep_mask = route_tokens(expert_ids, priority, num_experts, capacity)
        log_probs, router_probs, expert_onehot, gate_prob, mod_mask, local_stats = router_forward(x_loc, modality, router, expert_ids)
        aux_loss, mean_probs, mod_count = aux_from_stats(lax.psum(local_stats, ALL_AXES), num_experts)
        keep_col = keep_mask[:, None]
        slot_col = slot_valid[:, :, None]
        send_rows = jnp.where(slot_col, x_loc[slot_token], 0).astype(jnp.bfloat16)
        recv_rows = lax.all_to_all(send_rows, "ep", 0, 1, tiled=True)
        act_in = jnp.einsum("ecw,ewf->ecf", recv_rows, w_in, preferred_element_type=jnp.float32) + b_in[:, None, :].astype(jnp.float32)
        act_out, gelu_pullback = jax.vjp(jax.nn.gelu, act_in)
        hidden = act_out.astype(jnp.bfloat16)
        expert_out = jnp.einsum("ecf,efw->ecw", hidden, w_out, preferred_element_type=jnp.float32) + b_out[:, None, :].astype(jnp.float32)
        back_rows = lax.all_to_all(expert_out.astype(jnp.bfloat16), "ep", 1, 0, tiled=True)
        y_tok = back_rows.reshape(num_experts * capacity, model_width)[token_slot].astype(jnp.float32)
        out_tokens = jnp.where(keep_col, gate_prob[:, None] * y_tok, 0.0).astype(jnp.bfloat16)
        dy_f32 = dy_loc.astype(jnp.float32)
        d_gate = jnp.where(keep_mask, jnp.sum(dy_f32 * y_tok, axis=-1), 0.0)
        d_ytok = jnp.where(keep_col, gate_prob[:, None] * dy_f32, 0.0).astype(jnp.bfloat16)
        d_send = jnp.where(slot_col, d_ytok[slot_token], 0).astype(jnp.bfloat16)
        d_recv = lax.all_to_all(d_send, "ep", 0, 1, tiled=True)
        d_b_out = jnp.sum(d_recv.astype(jnp.float32), axis=1)
        d_w_out = jnp.einsum("ecf,ecw->efw", hidden, d_recv, preferred_element_type=jnp.float32)
        d_hidden = jnp.einsum("ecw,efw->ecf", d_recv, w_out, preferred_element_type=jnp.float32).astype(jnp.bfloat16)
        d_act = gelu_pullback(d_hidden.astype(jnp.float32))[0]
        d_b_in = jnp.sum(d_act, axis=1)
        d_act_bf = d_act.astype(jnp.bfloat16)
        d_w_in = jnp.einsum("ecw,ecf->ewf", recv_rows, d_act_bf, preferred_element_type=jnp.float32)
        d_rows = jnp.einsum("ecf,ewf->ecw", d_act_bf, w_in, preferred_element_type=jnp.float32).astype(jnp.bfloat16)
        d_back = lax.all_to_all(d_rows, "ep", 1, 0, tiled=True)
        dx_expert = jnp.where(keep_col, d_back.reshape(num_experts * capacity, model_width)[token_slot], 0).astype(jnp.bfloat16)
        d_router_part, dx_router = router_backward(x_loc, router, log_probs, router_probs, expert_onehot, mod_mask, mean_probs, mod_count, d_gate)
        d_router = lax.psum(d_router_part, ALL_AXES)
        expert_grads = lax.psum((d_w_in, d_b_in, d_w_out, d_b_out), "dp")
        return (out_tokens, aux_loss, dx_expert + dx_router, d_router) + tuple(grad_sum.astype(jnp.bfloat16) for grad_sum in expert_grads)

    return jax.shard_map(
        local_step,
        mesh=mesh,
        in_specs=(token_spec, token_spec, P(), token_spec, token_spec, expert_spec, expert_spec, expert_spec, expert_spec, token_spec),
        out_specs=(token_spec, P(), token_spec, P(), expert_spec, expert_spec, expert_spec, expert_spec),
        check_vma=False,
    )
```

profile of v0, /device:TPU:0, one launch (start us, length us, event | category | flops | bytes accessed | tf_op | source)
XLA Modules:
  0.0 2208.1 jit_solution(10582540041848143575)
XLA Ops:
  2.9 6.8 sort.31
  9.6 45.5 %gather_fusion = s32[8192]{0:T(1024)S(1)} fusion(s32[8192]{0:T(1024)S(1)} %get-tuple-element.10, s32[8192]{0:T(1024)S(1)} %broadcast_clamp_fusion), kind=kCustom, calls=%fused_computation | custom fusion | bytes 98304 | tf_op jit(solution)/shard_map/gather | solution.py:16
  55.2 43.2 %gather_fusion.1 = bf16[8192,768]{1,0:T(8,128)(2,1)} fusion(bf16[8192,768]{1,0:T(8,128)(2,1)} %param.10, s32[8192]{0:T(1024)S(1)} %broadcast_clamp_fusion.1), kind=kCustom, calls=%fused_computation.1 | custom fusion | bytes 25198592 | tf_op jit(solution)/shard_map/gather | solution.py:67
  98.5 10.9 broadcast_select_fusion.1
  115.6 139.7 %all-to-all-done = bf16[16,512,768]{2,1,0:T(8,128)(2,1)} async-done(((bf16[16,512,768]{2,1,0:T(8,128)(2,1)}), bf16[16,512,768]{2,1,0:T(8,128)(2,1)}, u32[]{:S(2)}, u32[]{:S(2)}) %all-to-all-start) | async-done | bytes 12582944 | tf_op jit(solution)/shard_map/all_to_all | solution.py:68
  255.3 10.6 copy.46
  265.9 75.4 %multiply_convert_fusion = (bf16[2,4096,3072]{2,1,0:T(8,128)(2,1)}, f32[2,4096,3072]{2,1,0:T(8,128)}) fusion(f32[2,3072]{1,0:T(2,128)S(1)} %convert_element_type.70, bf16[2,4096,768]{2,1,0:T(8,128)(2,1)} %bitcast.80, bf16[2,768,3072]{2,1,0:T(8,128)(2,1)} %param.15), kind=kOutput, calls=%fused_computation.18 | convolution fusion | flops 38906363904 | bytes 173039616 | tf_op jit(solution)/shard_map/ecw,ewf->ecf/dot_general | solution.py:69
  341.2 45.5 %add_convert_fusion = bf16[2,4096,768]{2,1,0:T(8,128)(2,1)S(1)} fusion(f32[2,768]{1,0:T(2,128)S(1)} %convert_element_type.72, bf16[2,4096,3072]{2,1,0:T(8,128)(2,1)} %get-tuple-element.48, bf16[2,3072,768]{2,1,0:T(8,128)(2,1)} %param.17), kind=kOutput, calls=%fused_computation.32 | convolution fusion | flops 38667288576 | bytes 72357888 | tf_op jit(solution)/shard_map/ecf,efw->ecw/dot_general | solution.py:72
  386.8 88.8 %copy.47 = bf16[2,4096,768]{2,0,1:T(2,128)(2,1)} copy(bf16[2,4096,768]{2,1,0:T(8,128)(2,1)S(1)} %add_convert_fusion) | data formatting | bytes 25165824 | tf_op jit(solution)/shard_map/convert_element_type | solution.py:73
  480.9 12.8 fusion.36
  495.1 150.3 %psum.42 = f32[2,18]{1,0:T(2,128)S(1)} all-reduce(f32[2,18]{1,0:T(2,128)S(1)} %pad_maximum_fusion), channel_id=1, replica_groups=mesh['dp'=2,'ep'=8] {'dp','ep'}, use_global_device_ids=true, to_apply=%region_9.10 | all-reduce | flops 36 | bytes 288 | tf_op jit(solution)/shard_map/psum | solution.py:64
  645.3 6.8 sort.32
  653.2 10.1 fusion.29
  663.4 11.7 copy.48
  675.1 43.3 %gather_fusion.2 = bf16[8192,768]{1,0:T(8,128)(2,1)} fusion(bf16[8192,768]{1,0:T(8,128)(2,1)} %bitcast.77, s32[8192]{0:T(1024)S(1)} %get-tuple-element.24), kind=kCustom, calls=%fused_computation.2 | custom fusion | bytes 25198592 | tf_op jit(solution)/shard_map/gather | solution.py:74
  718.4 10.5 fusion.13
  730.4 15.6 fusion.12
  746.1 43.5 %gather_fusion.3 = bf16[8192,768]{1,0:T(8,128)(2,1)} fusion(bf16[8192,768]{1,0:T(8,128)(2,1)} %get-tuple-element.26, s32[8192]{0:T(1024)S(1)} %copy-done.16), kind=kCustom, calls=%fused_computation.3 | custom fusion | bytes 25198592 | tf_op jit(solution)/shard_map/gather | solution.py:79
  789.6 10.9 broadcast_select_fusion
  808.4 8.0 convolution_bitcast_fusion
  816.4 154.4 %psum.43 = f32[768,16]{0,1:T(8,128)} all-reduce(f32[768,16]{0,1:T(8,128)S(1)} %convolution_bitcast_fusion), channel_id=1, replica_groups=mesh['dp'=2,'ep'=8] {'dp','ep'}, use_global_device_ids=true, to_apply=%region_14.15 | all-reduce | flops 12288 | bytes 98304 | tf_op jit(solution)/shard_map/psum | solution.py:92
  970.8 10.6 copy.51
  981.4 6.9 convert_reduce_fusion
  988.2 48.5 %fusion.38 = f32[2,3072,768]{2,1,0:T(8,128)} fusion(bf16[2,4096,3072]{2,1,0:T(8,128)(2,1)} %get-tuple-element.48, bf16[2,4096,768]{2,1,0:T(8,128)(2,1)} %bitcast.82), kind=kOutput, calls=%fused_computation.89 | convolution fusion | flops 38654705664 | bytes 81788928 | tf_op jit(solution)/shard_map/ecf,ecw->efw/dot_general | solution.py:82
  1036.8 105.7 %fusion.37 = (f32[2,3072]{1,0:T(2,128)S(1)}, bf16[2,4096,3072]{2,1,0:T(8,128)(2,1)}) fusion(f32[2,4096,3072]{2,1,0:T(8,128)} %get-tuple-element.49, f32[2,3072]{1,0:T(2,128)S(1)} %copy-done.27, bf16[2,4096,768]{2,1,0:T(8,128)(2,1)} %bitcast.83, bf16[2,3072,768]{2,1,0:T(8,128)(2,1)} %param.17), kind=kOutput, calls=%fused_computation.88 | convolution fusion | flops 39258677248 | bytes 173064192 | tf_op jit(solution)/shard_map/ecw,efw->ecf/dot_general | solution.py:83
  1142.5 49.2 %fusion.14 = f32[2,768,3072]{2,1,0:T(8,128)} fusion(bf16[2,4096,768]{2,1,0:T(8,128)(2,1)} %bitcast.81, bf16[2,4096,3072]{2,1,0:T(8,128)(2,1)} %get-tuple-element.52), kind=kOutput, calls=%fused_computation.28 | convolution fusion | flops 38654705664 | bytes 81788928 | tf_op jit(solution)/shard_map/ecw,ecf->ewf/dot_general | solution.py:87
  1191.7 47.5 %fusion.18 = bf16[2,4096,768]{2,1,0:T(8,128)(2,1)} fusion(bf16[2,768,3072]{2,1,0:T(8,128)(2,1)} %param.15, bf16[2,4096,3072]{2,1,0:T(8,128)(2,1)} %get-tuple-element.52), kind=kOutput, calls=%fused_computation.37 | convolution fusion | flops 38660997120 | bytes 72351744 | tf_op jit(solution)/shard_map/ecf,ewf->ecw/dot_general | solution.py:88
  1239.2 23.8 %copy.52 = bf16[2,4096,768]{2,0,1:T(2,128)(2,1)} copy(bf16[2,4096,768]{2,1,0:T(8,128)(2,1)} %fusion.18) | data formatting | bytes 25165824 | tf_op jit(solution)/shard_map/convert_element_type | solution.py:88
  1268.6 857.7 %all-reduce.2 = (bf16[2,768,3072]{2,1,0:T(8,128)(2,1)}, bf16[2,3072]{1,0:T(2,128)(2,1)}, bf16[2,3072,768]{2,1,0:T(8,128)(2,1)}, bf16[2,768]{1,0:T(2,128)(2,1)}) all-reduce(f32[2,768,3072]{2,1,0:T(8,128)} %fusion.14, f32[2,3072]{1,0:T(2,128)S(1)} %get-tuple-element.51, ...), channel_id=1, replica_groups=mesh['dp'=2,'ep'=8] {'dp'}, use_global_device_ids=true, to_apply=%region_15.16 | all-reduce | flops 9444864 | bytes 56669184 | tf_op jit(solution)/shard_map/psum | solution.py:93
  2126.3 11.9 copy.53
  2138.2 43.4 %gather_fusion.4 = bf16[8192,768]{1,0:T(8,128)(2,1)} fusion(bf16[8192,768]{1,0:T(8,128)(2,1)} %bitcast.76, s32[8192]{0:T(1024)S(1)} %copy-done.14), kind=kCustom, calls=%fused_computation.4 | custom fusion | bytes 25198592 | tf_op jit(solution)/shard_map/gather | solution.py:90
  2181.6 25.1 %select_add_fusion = bf16[8192,768]{1,0:T(8,128)(2,1)} fusion(bf16[8192,768]{1,0:T(8,128)(2,1)} %gather_fusion.4, pred[8192]{0:T(1024)(128)(4,1)S(1)} %copy-done.24, f32[768,16]{0,1:T(8,128)S(1)} %copy-done, f32[8192,16]{0,1:T(8,128)S(1)} %copy-done.7, f32[8192]{0:T(1024)S(1)} %copy-done.20, f32[8192,16]{0,1:T(8,128)S(1)} %copy-done.5, ...), kind=kOutput, calls=%fused_computation.34 | convolution fusion | flops 1227358208 | bytes 26370048 | tf_op jit(solution)/shard_map/te,we->tw/dot_general | solution.py:50
  (106 shorter events, 29.8 us)
Async XLA Ops:
  0.6 480.2 %copy-start = (f32[768,16]{0,1:T(8,128)S(1)}, f32[768,16]{0,1:T(8,128)}, u32[]{:S(2)}) copy-start(f32[768,16]{0,1:T(8,128)} %param.12) | copy-start | bytes 147460
  1.7 96.8 %copy-start.21 = (pred[16,512]{1,0:T(8,128)(4,1)}, pred[16,512]{1,0:T(8,128)(4,1)S(1)}, u32[]{:S(2)}) copy-start(pred[16,512]{1,0:T(8,128)(4,1)S(1)} %iota_compare_fusion.1) | copy-start | bytes 24580
  9.6 45.5 %copy-start.1 = (s32[8192]{0:T(1024)}, s32[8192]{0:T(1024)S(1)}, u32[]{:S(2)}) copy-start(s32[8192]{0:T(1024)S(1)} %get-tuple-element.10) | copy-start | bytes 98308
  55.2 43.3 %copy-start.15 = (s32[8192]{0:T(1024)}, s32[8192]{0:T(1024)S(1)}, u32[]{:S(2)}) copy-start(s32[8192]{0:T(1024)S(1)} %broadcast_clamp_fusion.1) | copy-start | bytes 98308
  109.4 6.2 copy-start.30
  109.4 145.9 %all-to-all-start = ((bf16[16,512,768]{2,1,0:T(8,128)(2,1)}), bf16[16,512,768]{2,1,0:T(8,128)(2,1)}, u32[]{:S(2)}, u32[]{:S(2)}) async-start(bf16[16,512,768]{2,1,0:T(8,128)(2,1)} %broadcast_select_fusion.1), calls=%async_computation | async-start | bytes 25165824 | tf_op jit(solution)/shard_map/all_to_all | solution.py:68
  115.6 150.3 %copy-start.26 = (f32[2,3072]{1,0:T(2,128)}, f32[2,3072]{1,0:T(2,128)S(1)}, u32[]{:S(2)}) copy-start(f32[2,3072]{1,0:T(2,128)S(1)} %convert_element_type.70) | copy-start | bytes 73732
  475.5 187.9 %all-to-all-start.1 = ((bf16[2,4096,768]{2,0,1:T(2,128)(2,1)}), bf16[2,4096,768]{2,0,1:T(2,128)(2,1)}, u32[]{:S(2)}, u32[]{:S(2)}) async-start(bf16[2,4096,768]{2,0,1:T(2,128)(2,1)} %copy.47), calls=%async_computation.1 | async-start | bytes 25165824 | tf_op jit(solution)/shard_map/all_to_all | solution.py:73
  480.9 13.0 copy-start.25
  480.9 164.4 %copy-start.2 = (s32[8192]{0:T(1024)S(1)}, s32[8192]{0:T(1024)}, u32[]{:S(2)}) copy-start(s32[8192]{0:T(1024)} %copy-done.1) | copy-start | bytes 98308
  480.9 171.4 %copy-start.18 = (s32[16]{0:T(128)S(1)}, s32[16]{0:T(128)}, u32[]{:S(2)}) copy-start(s32[16]{0:T(128)} %copy-done.17) | copy-start | bytes 196
  480.9 172.3 %copy-start.12 = (s32[8192]{0:T(1024)S(1)}, s32[8192]{0:T(1024)}, u32[]{:S(2)}) copy-start(s32[8192]{0:T(1024)} %param.13) | copy-start | bytes 98308
  493.7 314.6 %copy-start.4 = (f32[8192,16]{0,1:T(8,128)}, f32[8192,16]{0,1:T(8,128)S(1)}, u32[]{:S(2)}) copy-start(f32[8192,16]{0,1:T(8,128)S(1)} %get-tuple-element.47) | copy-start | bytes 1572868
  493.8 314.6 %copy-start.8 = (f32[8192]{0:T(1024)}, f32[8192]{0:T(1024)S(1)}, u32[]{:S(2)}) copy-start(f32[8192]{0:T(1024)S(1)} %get-tuple-element.46) | copy-start | bytes 98308
  493.9 314.4 %copy-start.10 = (f32[8192]{0:T(1024)}, f32[8192]{0:T(1024)S(1)}, u32[]{:S(2)}) copy-start(f32[8192]{0:T(1024)S(1)} %log.13) | copy-start | bytes 98308
  663.4 11.7 copy-start.13
  718.4 12.0 copy-start.3
  728.9 17.1 copy-start.23
  729.5 78.9 %copy-start.6 = (f32[8192,16]{0,1:T(8,128)}, f32[8192,16]{0,1:T(8,128)S(1)}, u32[]{:S(2)}) copy-start(f32[8192,16]{0,1:T(8,128)S(1)} %get-tuple-element.50) | copy-start | bytes 1572868
  729.5 78.9 %copy-start.19 = (f32[8192]{0:T(1024)}, f32[8192]{0:T(1024)S(1)}, u32[]{:S(2)}) copy-start(f32[8192]{0:T(1024)S(1)} %get-tuple-element.12) | copy-start | bytes 98308
  730.4 15.6 copy-start.16
  746.1 43.5 %copy-start.22 = (pred[16,512]{1,0:T(8,128)(4,1)S(1)}, pred[16,512]{1,0:T(8,128)(4,1)}, u32[]{:S(2)}) copy-start(pred[16,512]{1,0:T(8,128)(4,1)} %copy-done.21) | copy-start | bytes 24580
  800.4 170.3 %all-to-all-start.2 = ((bf16[16,512,768]{2,1,0:T(8,128)(2,1)}), bf16[16,512,768]{2,1,0:T(8,128)(2,1)}, u32[]{:S(2)}, u32[]{:S(2)}) async-start(bf16[16,512,768]{2,1,0:T(8,128)(2,1)} %broadcast_select_fusion), calls=%async_computation.2 | async-start | bytes 25165824 | tf_op jit(solution)/shard_map/all_to_all | solution.py:80
  988.2 48.5 %copy-start.27 = (f32[2,3072]{1,0:T(2,128)S(1)}, f32[2,3072]{1,0:T(2,128)}, u32[]{:S(2)}) copy-start(f32[2,3072]{1,0:T(2,128)} %copy-done.26) | copy-start | bytes 73732
  1263.0 863.2 %all-to-all-start.3 = ((bf16[2,4096,768]{2,0,1:T(2,128)(2,1)}), bf16[2,4096,768]{2,0,1:T(2,128)(2,1)}, u32[]{:S(2)}, u32[]{:S(2)}) async-start(bf16[2,4096,768]{2,0,1:T(2,128)(2,1)} %copy.52), calls=%async_computation.3 | async-start | bytes 25165824 | tf_op jit(solution)/shard_map/all_to_all | solution.py:89
  2126.3 11.9 copy-start.14
  2138.2 43.4 %copy-start.5 = (f32[8192,16]{0,1:T(8,128)S(1)}, f32[8192,16]{0,1:T(8,128)}, u32[]{:S(2)}) copy-start(f32[8192,16]{0,1:T(8,128)} %copy-done.4) | copy-start | bytes 1572868
  2138.2 43.4 %copy-start.7 = (f32[8192,16]{0,1:T(8,128)S(1)}, f32[8192,16]{0,1:T(8,128)}, u32[]{:S(2)}) copy-start(f32[8192,16]{0,1:T(8,128)} %copy-done.6) | copy-start | bytes 1572868
  2138.2 43.4 %copy-start.9 = (f32[8192]{0:T(1024)S(1)}, f32[8192]{0:T(1024)}, u32[]{:S(2)}) copy-start(f32[8192]{0:T(1024)} %copy-done.8) | copy-start | bytes 98308
  2138.2 43.4 %copy-start.11 = (f32[8192]{0:T(1024)S(1)}, f32[8192]{0:T(1024)}, u32[]{:S(2)}) copy-start(f32[8192]{0:T(1024)} %copy-done.10) | copy-start | bytes 98308
  2138.2 43.4 %copy-start.20 = (f32[8192]{0:T(1024)S(1)}, f32[8192]{0:T(1024)}, u32[]{:S(2)}) copy-start(f32[8192]{0:T(1024)} %copy-done.19) | copy-start | bytes 98308
  2138.2 43.4 %copy-start.24 = (pred[8192]{0:T(1024)(128)(4,1)S(1)}, pred[8192]{0:T(1024)(128)(4,1)}, u32[]{:S(2)}) copy-start(pred[8192]{0:T(1024)(128)(4,1)} %copy-done.23) | copy-start | bytes 24580
  (3 other events, 12.6 us)
where the time goes:
time: 2210 us
  blocking collectives  1160 us (52%)
  matrix products  419 us (19%)
  local copies, waits for them, and re-layouts  378 us (17%)
  waiting for transfers between devices  140 us (6%)
  other arithmetic  82.5 us (4%)
  starting transfers between devices  22.3 us (1%)
    psum x1, blocking collectives, local_step(): expert_grads = lax.psum((d_w_in, d_b_in, d_w_out, d_b_out), 'dp')  858 us
    psum x1, blocking collectives, local_step(): d_router = lax.psum(d_router_part, ALL_AXES)  154 us
    psum x1, blocking collectives, local_step(): lax.psum(local_stats, ALL_AXES)  150 us
    all_to_all x1, waiting for transfers between devices, local_step(): recv_rows = lax.all_to_all(send_rows, 'ep', 0, 1, tiled=True)  140 us
    dot_general x1, matrix products, local_step(): jnp.einsum('ecw,efw->ecf', d_recv, w_out, preferred_element_type=jnp.floa...  106 us
    convert_element_type x1, local copies, waits for them, and re-layouts, local_step(): expert_out.astype(jnp.bfloat16)  88.8 us
    dot_general x1, matrix products, local_step(): jnp.einsum('ecw,ewf->ecf', recv_rows, w_in, preferred_element_type=jnp.fl...  75.4 us
    dot_general x1, matrix products, local_step(): jnp.einsum('ecw,ecf->ewf', recv_rows, d_act_bf, preferred_element_type=jn...  49.2 us
  transfers between devices with their start and end apart: 4, of which 1 were waited for; matrix products, arithmetic and copies ran while one was open for 2% of the time, Pallas kernels for 0%

commit v1 on v0

v1 whole, which is shorter than its diff:
```python
import functools
import jax
import jax.numpy as jnp
from jax import lax
from jax.experimental import pallas as pl
from jax.experimental.pallas import tpu as pltpu
from jax.sharding import PartitionSpec as P

F32 = jnp.float32
BF16 = jnp.bfloat16
VMEM_CAP = 66_000_000
GELU_SCALE = 0.7978845608028654
GELU_CUBE = 0.044715
FCHUNK = 768


def gelu_and_slope(a):
    sq = a * a
    t = jnp.tanh(GELU_SCALE * (a + GELU_CUBE * (a * sq)))
    cdf = 0.5 * (1.0 + t)
    slope = cdf + (0.5 * a) * ((1.0 - t * t) * (GELU_SCALE * (1.0 + (3.0 * GELU_CUBE) * sq)))
    return a * cdf, slope


def expert_body(want_rows, dw_in_init, dw_final, nsteps, fchunk, *refs):
    it = iter(refs)
    sel_ref = next(it)
    x_ref, d_ref, w1_ref, b1_ref, w2_ref, b2_ref = (next(it) for _ in range(6))
    want_dw = dw_final is not None
    if dw_in_init:
        p1_ref, p2_ref, pb1_ref, pb2_ref = (next(it) for _ in range(4))
    if want_rows:
        y_ref, dx_ref = next(it), next(it)
    if want_dw:
        g1_ref, g2_ref, gb1_ref, gb2_ref = (next(it) for _ in range(4))
        acc1, acc2, xt, dt, sem = (next(it) for _ in range(5))
        if dw_final:
            stage = next(it)
    if want_rows:
        yacc, dxacc = next(it), next(it)
    step = pl.program_id(0)
    width = x_ref.shape[-1]
    hidden = w1_ref.shape[-1]
    x = x_ref[...].reshape(-1, width)
    d = d_ref[...].reshape(-1, width)
    if want_dw:
        @pl.when(step == 0)
        def _():
            if dw_in_init:
                c1 = pltpu.make_async_copy(p1_ref, acc1, sem.at[0])
                c2 = pltpu.make_async_copy(p2_ref, acc2, sem.at[1])
                c1.start()
                c2.start()
                gb1_ref[...] = pb1_ref[...]
                gb2_ref[...] = pb2_ref[...]
                c1.wait()
                c2.wait()
            else:
                acc1[...] = jnp.zeros_like(acc1)
                acc2[...] = jnp.zeros_like(acc2)
                gb1_ref[...] = jnp.zeros_like(gb1_ref)
                gb2_ref[...] = jnp.zeros_like(gb2_ref)

        xt[...] = x.T
        dt[...] = d.T
        gb2_ref[...] += jnp.sum(d.astype(F32), axis=0, keepdims=True)
    if want_rows:
        yacc[...] = jnp.broadcast_to(b2_ref[0].astype(F32), yacc.shape)
        dxacc[...] = jnp.zeros_like(dxacc)

    def chunk(j, carry):
        cols = pl.ds(pl.multiple_of(j * fchunk, fchunk), fchunk)
        w1 = w1_ref[0, :, cols]
        w2 = w2_ref[0, cols, :]
        a = jnp.dot(x, w1, preferred_element_type=F32) + b1_ref[0, :, cols].astype(F32)
        dh = lax.dot_general(d, w2, (((1,), (1,)), ((), ())), preferred_element_type=F32)
        h, slope = gelu_and_slope(a)
        da = dh.astype(BF16).astype(F32) * slope
        h16 = h.astype(BF16)
        da16 = da.astype(BF16)
        if want_rows:
            yacc[...] += jnp.dot(h16, w2, preferred_element_type=F32)
            dxacc[...] += lax.dot_general(da16, w1, (((1,), (1,)), ((), ())), preferred_element_type=F32)
        if want_dw:
            gb1_ref[:, cols] += jnp.sum(da, axis=0, keepdims=True)
            acc1[:, cols] += jnp.dot(xt[...], da16, preferred_element_type=F32)
            acc2[:, cols] += jnp.dot(dt[...], h16, preferred_element_type=F32)
        return carry

    lax.fori_loop(0, hidden // fchunk, chunk, 0)
    if want_rows:
        y_ref[...] = yacc[...].astype(BF16).reshape(y_ref.shape)
        dx_ref[...] = dxacc[...].astype(BF16).reshape(dx_ref.shape)
    if want_dw:
        @pl.when(step == nsteps - 1)
        def _():
            if dw_final:
                def put(j, carry):
                    cols = pl.ds(pl.multiple_of(j * fchunk, fchunk), fchunk)
                    stage[...] = acc2[:, cols].T.astype(BF16)
                    c = pltpu.make_async_copy(stage, g2_ref.at[cols, :], sem.at[1])
                    c.start()
                    c.wait()
                    stage[...] = acc1[:, cols].astype(BF16)
                    c = pltpu.make_async_copy(stage, g1_ref.at[:, cols], sem.at[0])
                    c.start()
                    c.wait()
                    return carry

                lax.fori_loop(0, hidden // fchunk, put, 0)
            else:
                c1 = pltpu.make_async_copy(acc1, g1_ref, sem.at[0])
                c2 = pltpu.make_async_copy(acc2, g2_ref, sem.at[1])
                c1.start()
                c2.start()
                c1.wait()
                c2.wait()


def expert_call(sel, rows, cots, w1, b1, w2, b2, partial=None, want_rows=True, dw=None, fchunk=FCHUNK):
    tiles, r, width = rows.shape
    hidden = w1.shape[-1]
    one = pl.Buffered(1)
    tile = pl.BlockSpec((1, r, width), lambda i, s: (i, 0, 0))
    anyspec = pl.BlockSpec(memory_space=pl.ANY)
    vec1 = pl.BlockSpec((1, hidden), lambda i, s: (0, 0))
    vec2 = pl.BlockSpec((1, width), lambda i, s: (0, 0))
    in_specs = [
        tile, tile,
        pl.BlockSpec((1, width, hidden), lambda i, s: (s[0], 0, 0), pipeline_mode=one),
        pl.BlockSpec((1, 1, hidden), lambda i, s: (s[0], 0, 0)),
        pl.BlockSpec((1, hidden, width), lambda i, s: (s[0], 0, 0), pipeline_mode=one),
        pl.BlockSpec((1, 1, width), lambda i, s: (s[0], 0, 0)),
    ]
    args = [rows, cots, w1, b1[:, None, :], w2, b2[:, None, :]]
    if partial is not None:
        in_specs += [anyspec, anyspec, vec1, vec2]
        args += list(partial)
    out_shape, out_specs, scratch = [], [], []
    if want_rows:
        out_shape += [jax.ShapeDtypeStruct(rows.shape, BF16)] * 2
        out_specs += [tile, tile]
    if dw:
        t = F32 if dw == "partial" else BF16
        g2 = (width, hidden) if dw == "partial" else (hidden, width)
        out_shape += [jax.ShapeDtypeStruct((width, hidden), t), jax.ShapeDtypeStruct(g2, t),
                      jax.ShapeDtypeStruct((1, hidden), F32), jax.ShapeDtypeStruct((1, width), F32)]
        out_specs += [anyspec, anyspec, vec1, vec2]
        scratch += [pltpu.VMEM((width, hidden), F32), pltpu.VMEM((width, hidden), F32),
                    pltpu.VMEM((width, r), BF16), pltpu.VMEM((width, r), BF16), pltpu.SemaphoreType.DMA((2,))]
        if dw == "final":
            assert fchunk == width
            scratch += [pltpu.VMEM((fchunk, width), BF16)]
    if want_rows:
        scratch += [pltpu.VMEM((r, width), F32), pltpu.VMEM((r, width), F32)]
    dots = 2 + 2 * bool(want_rows) + 2 * bool(dw)
    flops = dots * 2 * tiles * r * width * hidden
    body = functools.partial(expert_body, want_rows, partial is not None, None if not dw else dw == "final", tiles, fchunk)
    return pl.pallas_call(
        body,
        grid_spec=pltpu.PrefetchScalarGridSpec(num_scalar_prefetch=1, grid=(tiles,), in_specs=in_specs, out_specs=out_specs, scratch_shapes=scratch),
        out_shape=out_shape,
        compiler_params=pltpu.CompilerParams(vmem_limit_bytes=VMEM_CAP, dimension_semantics=("arbitrary",)),
        cost_estimate=pl.CostEstimate(flops=flops, bytes_accessed=4 * tiles * r * width * 2, transcendentals=tiles * r * hidden),
        name="expert_" + ("rows" if want_rows else "") + (dw or ""),
    )(sel, *args)


ALL_AXES = ("dp", "ep")
MESH_ID = pl.DeviceIdType.MESH


def slots_kernel(num_tokens, capacity, scal_ref, order_ref, xs_ref, ds_ref):
    mine = lax.axis_index("dp")
    experts = xs_ref.shape[0] * 128 // capacity
    rows = capacity // 128
    lane = lax.broadcasted_iota(jnp.int32, (rows, 128), 1)
    rank = lax.broadcasted_iota(jnp.int32, (rows, 128), 0) * 128 + lane
    for j in range(experts):
        owner = (1 - mine) if j < experts // 2 else mine
        e = 2 * (j % (experts // 2)) + owner
        start = scal_ref[e]
        count = scal_ref[experts + e]
        block = order_ref[pl.ds(start // 128, 8), :]
        off = lax.rem(start, 128)
        turned = pltpu.roll(block, lax.rem(128 - off, 128), 1)
        tok = jnp.where(lane < 128 - off, turned[:rows], turned[1:rows + 1])
        xs_ref[rows * j:rows * (j + 1), :] = jnp.where(rank < count, tok, 0)
        ds_ref[rows * j:rows * (j + 1), :] = jnp.where(rank < count, tok, num_tokens)


def slot_tables(order, starts, counts, capacity):
    num_tokens = order.shape[0]
    experts = starts.shape[0]
    padded = jnp.pad(order, (0, 1024)).reshape(-1, 128)
    shape = jax.ShapeDtypeStruct((experts * capacity // 128, 128), jnp.int32)
    xs, ds = pl.pallas_call(
        functools.partial(slots_kernel, num_tokens, capacity),
        in_specs=[pl.BlockSpec(memory_space=pltpu.SMEM), pl.BlockSpec(memory_space=pltpu.VMEM)],
        out_specs=[pl.BlockSpec(memory_space=pltpu.VMEM)] * 2,
        out_shape=[shape, shape],
        cost_estimate=pl.CostEstimate(flops=1_000_000, bytes_accessed=200_000, transcendentals=0),
        name="slots",
    )(jnp.concatenate([starts, counts]), padded)
    half = experts * capacity // 2
    xs, ds = xs.reshape(-1), ds.reshape(-1)
    return (xs[:half], xs[half:]), (ds[:half], ds[half:])


def sum_kernel(ep_size, count, x_ref, out_ref, slots, send_sem, recv_sem):
    dp_me, ep_me = lax.axis_index("dp"), lax.axis_index("ep")
    me = dp_me * ep_size + ep_me

    def peer(k):
        p = lax.rem(me + k, count)
        return (p // ep_size, lax.rem(p, ep_size))

    barrier = pltpu.get_barrier_semaphore()
    for k in range(1, count):
        pl.semaphore_signal(barrier, inc=1, device_id=peer(k), device_id_type=MESH_ID)
    pl.semaphore_wait(barrier, count - 1)
    copies = []
    for k in range(1, count):
        c = pltpu.make_async_remote_copy(
            src_ref=x_ref, dst_ref=slots.at[me], send_sem=send_sem.at[k], recv_sem=recv_sem.at[k],
            device_id=peer(k), device_id_type=MESH_ID)
        c.start()
        copies.append(c)
    slots[me] = x_ref[...]
    for c in copies:
        c.wait()
    total = slots[0]
    for k in range(1, count):
        total = total + slots[k]
    out_ref[...] = total


def device_sum(x, mesh, collective_id):
    count = mesh.shape["dp"] * mesh.shape["ep"]
    return pl.pallas_call(
        functools.partial(sum_kernel, mesh.shape["ep"], count),
        in_specs=[pl.BlockSpec(memory_space=pltpu.VMEM)],
        out_specs=pl.BlockSpec(memory_space=pltpu.VMEM),
        out_shape=jax.ShapeDtypeStruct(x.shape, F32),
        scratch_shapes=[pltpu.VMEM((count,) + x.shape, F32), pltpu.SemaphoreType.DMA((count,)), pltpu.SemaphoreType.DMA((count,))],
        compiler_params=pltpu.CompilerParams(collective_id=collective_id, has_side_effects=True),
        cost_estimate=pl.CostEstimate(flops=10_000_000, bytes_accessed=1_000_000, transcendentals=0),
        name="device_sum",
    )(x)


def exchange_body(ep_size, count, fchunk,
                  xs, ds, xo, do, w1_hbm, w2_hbm, b1_ref, b2_ref, st_ref,
                  yb, dxb, g1_ref, g2_ref, gb1_ref, gb2_ref, st_out, xr, dr, xf, df, yl, dxl,
                  w1, w2, acc1, acc2, xv, dv, xt, dt, yacc, dxacc, ystage, dxstage, stage, slots,
                  st_send, st_recv, x_send, x_recv, d_send, d_recv, xf_send, xf_recv, df_send, df_recv,
                  y_send, y_recv, dx_send, dx_recv, w_sem, in_sem, out_sem):
    width = w1.shape[0]
    hidden = w1.shape[1]
    mine, e = lax.axis_index("dp"), lax.axis_index("ep")
    me = mine * ep_size + e

    def anyone(k):
        p = lax.rem(me + k, count)
        return (p // ep_size, lax.rem(p, ep_size))

    def dest(k):
        return lax.rem(e + k, ep_size)

    def source(k):
        return lax.rem(e + ep_size - k, ep_size)

    def remote(src, dst, send, recv, dp, ep):
        return pltpu.make_async_remote_copy(src_ref=src, dst_ref=dst, send_sem=send, recv_sem=recv,
                                            device_id=(dp, ep), device_id_type=MESH_ID)

    def stat_copy(k):
        dp, ep = anyone(k)
        return remote(st_ref, slots.at[me], st_send.at[k], st_recv.at[k], dp, ep)

    def x_copy(k):
        return remote(xs.at[dest(k)], xr.at[e], x_send.at[k], x_recv.at[k], mine, dest(k))

    def d_copy(k):
        return remote(ds.at[dest(k)], dr.at[e], d_send.at[k], d_recv.at[k], mine, dest(k))

    def xf_copy(t):
        return remote(xo.at[t], xf.at[t], xf_send.at[t], xf_recv.at[t], 1 - mine, e)

    def df_copy(t):
        return remote(do.at[t], df.at[t], df_send.at[t], df_recv.at[t], 1 - mine, e)

    def y_copy(k):
        return remote(yl.at[source(k)], yb.at[e], y_send.at[k], y_recv.at[k], mine, source(k))

    def dx_copy(k):
        return remote(dxl.at[source(k)], dxb.at[e], dx_send.at[k], dx_recv.at[k], mine, source(k))

    load1 = pltpu.make_async_copy(w1_hbm.at[mine], w1, w_sem.at[0])
    load2 = pltpu.make_async_copy(w2_hbm.at[mine], w2, w_sem.at[1])
    load1.start()
    load2.start()
    barrier = pltpu.get_barrier_semaphore()
    for k in range(1, count):
        pl.semaphore_signal(barrier, inc=1, device_id=anyone(k), device_id_type=MESH_ID)
    pl.semaphore_wait(barrier, count - 1)
    for k in range(1, count):
        stat_copy(k).start()
    for k in range(1, ep_size):
        x_copy(k).start()
        d_copy(k).start()
    for t in range(ep_size):
        xf_copy(t).start()
        df_copy(t).start()
    slots[me] = st_ref[...]
    acc1[...] = jnp.zeros_like(acc1)
    acc2[...] = jnp.zeros_like(acc2)
    gb1_ref[...] = jnp.zeros_like(gb1_ref)
    gb2_ref[...] = jnp.zeros_like(gb2_ref)

    def fetch(x_src, d_src, slot):
        return (pltpu.make_async_copy(x_src, xv.at[slot], in_sem.at[0, slot]),
                pltpu.make_async_copy(d_src, dv.at[slot], in_sem.at[1, slot]))

    def start_all(copies):
        for c in copies:
            c.start()

    def wait_all(copies):
        for c in copies:
            c.wait()

    def tile(slot, want_rows):
        x, d = xv[slot], dv[slot]
        xt[...] = x.T
        dt[...] = d.T
        gb2_ref[...] += jnp.sum(d.astype(F32), axis=0, keepdims=True)
        if want_rows:
            yacc[...] = jnp.broadcast_to(b2_ref[mine].astype(F32), yacc.shape)
            dxacc[...] = jnp.zeros_like(dxacc)

        def chunk(j, carry):
            cols = pl.ds(pl.multiple_of(j * fchunk, fchunk), fchunk)
            w1c = w1[:, cols]
            w2c = w2[cols, :]
            a = jnp.dot(x, w1c, preferred_element_type=F32) + b1_ref[mine, :, cols].astype(F32)
            dh = lax.dot_general(d, w2c, (((1,), (1,)), ((), ())), preferred_element_type=F32)
            h, slope = gelu_and_slope(a)
            da = dh.astype(BF16).astype(F32) * slope
            h16 = h.astype(BF16)
            da16 = da.astype(BF16)
            if want_rows:
                yacc[...] += jnp.dot(h16, w2c, preferred_element_type=F32)
                dxacc[...] += lax.dot_general(da16, w1c, (((1,), (1,)), ((), ())), preferred_element_type=F32)
            gb1_ref[:, cols] += jnp.sum(da, axis=0, keepdims=True)
            acc1[:, cols] += jnp.dot(xt[...], da16, preferred_element_type=F32)
            acc2[:, cols] += jnp.dot(dt[...], h16, preferred_element_type=F32)
            return carry

        lax.fori_loop(0, hidden // fchunk, chunk, 0)

    first = fetch(xs.at[e], ds.at[e], 0)
    start_all(first)
    load1.wait()
    load2.wait()
    wait_all(first)

    def near_step(k, carry):
        slot = lax.rem(k, 2)
        src = source(k)

        @pl.when(k > 0)
        def _():
            wait_all(fetch(xr.at[src], dr.at[src], slot))

        tile(slot, True)

        @pl.when(k < ep_size - 1)
        def _():
            x_copy(k + 1).wait_recv()
            d_copy(k + 1).wait_recv()
            start_all(fetch(xr.at[source(k + 1)], dr.at[source(k + 1)], lax.rem(k + 1, 2)))

        @pl.when(k == ep_size - 1)
        def _():
            xf_copy(0).wait_recv()
            df_copy(0).wait_recv()
            start_all(fetch(xf.at[0], df.at[0], 0))

        ystage[...] = yacc[...].astype(BF16)
        dxstage[...] = dxacc[...].astype(BF16)

        @pl.when(k == 0)
        def _():
            out = (pltpu.make_async_copy(ystage, yb.at[e], out_sem.at[0]), pltpu.make_async_copy(dxstage, dxb.at[e], out_sem.at[1]))
            start_all(out)
            wait_all(out)

        @pl.when(k > 0)
        def _():
            out = (pltpu.make_async_copy(ystage, yl.at[src], out_sem.at[0]), pltpu.make_async_copy(dxstage, dxl.at[src], out_sem.at[1]))
            start_all(out)
            wait_all(out)
            y_copy(k).start()
            dx_copy(k).start()

        return carry

    lax.fori_loop(0, ep_size, near_step, 0)

    def far_step(t, carry):
        slot = lax.rem(t, 2)
        wait_all(fetch(xf.at[t], df.at[t], slot))

        tile(slot, False)

        @pl.when(t < ep_size - 1)
        def _():
            xf_copy(t + 1).wait_recv()
            df_copy(t + 1).wait_recv()
            start_all(fetch(xf.at[t + 1], df.at[t + 1], lax.rem(t + 1, 2)))

        return carry

    lax.fori_loop(0, ep_size, far_step, 0)

    def put(j, carry):
        cols = pl.ds(pl.multiple_of(j * fchunk, fchunk), fchunk)
        stage[0] = acc2[:, cols].T.astype(BF16)
        c2 = pltpu.make_async_copy(stage.at[0], g2_ref.at[cols, :], out_sem.at[1])
        c2.start()
        stage[1] = acc1[:, cols].astype(BF16)
        c1 = pltpu.make_async_copy(stage.at[1], g1_ref.at[:, cols], out_sem.at[0])
        c1.start()
        c2.wait()
        c1.wait()
        return carry

    lax.fori_loop(0, hidden // fchunk, put, 0)
    for k in range(1, count):
        stat_copy(k).wait()
    total = slots[0]
    for k in range(1, count):
        total = total + slots[k]
    st_out[...] = total
    for t in range(ep_size):
        xf_copy(t).wait_send()
        df_copy(t).wait_send()
    for k in range(1, ep_size):
        x_copy(k).wait_send()
        d_copy(k).wait_send()
        y_copy(k).wait()
        dx_copy(k).wait()


def exchange_call(mesh, xs, ds, xo, do, w1, b1, w2, b2, stats, fchunk=FCHUNK):
    ep_size = mesh.shape["ep"]
    count = mesh.shape["dp"] * ep_size
    tiles, r, width = xs.shape
    hidden = w1.shape[-1]
    anyspec = pl.BlockSpec(memory_space=pl.ANY)
    vm = pl.BlockSpec(memory_space=pltpu.VMEM)
    rows = jax.ShapeDtypeStruct(xs.shape, BF16)
    out_shape = [rows, rows, jax.ShapeDtypeStruct((width, hidden), BF16), jax.ShapeDtypeStruct((hidden, width), BF16),
                 jax.ShapeDtypeStruct((1, hidden), F32), jax.ShapeDtypeStruct((1, width), F32), jax.ShapeDtypeStruct(stats.shape, F32)] + [rows] * 6
    out_specs = [anyspec] * 4 + [vm] * 3 + [anyspec] * 6
    dma = pltpu.SemaphoreType.DMA
    scratch = [
        pltpu.VMEM((width, hidden), BF16), pltpu.VMEM((hidden, width), BF16),
        pltpu.VMEM((width, hidden), F32), pltpu.VMEM((width, hidden), F32),
        pltpu.VMEM((2, r, width), BF16), pltpu.VMEM((2, r, width), BF16),
        pltpu.VMEM((width, r), BF16), pltpu.VMEM((width, r), BF16),
        pltpu.VMEM((r, width), F32), pltpu.VMEM((r, width), F32),
        pltpu.VMEM((r, width), BF16), pltpu.VMEM((r, width), BF16),
        pltpu.VMEM((2, fchunk, width), BF16), pltpu.VMEM((count,) + stats.shape, F32),
        dma((count,)), dma((count,)),
    ] + [dma((ep_size,))] * 12 + [dma((2,)), dma((2, 2)), dma((2,))]
    flops = 10 * 2 * tiles * r * width * hidden
    return pl.pallas_call(
        functools.partial(exchange_body, ep_size, count, fchunk),
        in_specs=[anyspec] * 6 + [vm] * 3,
        out_specs=out_specs,
        out_shape=out_shape,
        scratch_shapes=scratch,
        compiler_params=pltpu.CompilerParams(vmem_limit_bytes=VMEM_CAP, collective_id=1, has_side_effects=True),
        cost_estimate=pl.CostEstimate(flops=flops, bytes_accessed=8 * tiles * r * width * 2, transcendentals=2 * tiles * r * hidden),
        name="exchange",
    )(xs, ds, xo, do, w1, w2, b1[:, None, :], b2[:, None, :], stats)[:7]


def router_forward(x_loc, modality, router, expert_ids):
    num_experts = router.shape[1]
    logits = jnp.dot(x_loc, router, precision=lax.Precision.HIGHEST, preferred_element_type=F32)
    log_probs = jax.nn.log_softmax(logits, axis=-1)
    router_probs = jnp.exp(log_probs)
    expert_onehot = (expert_ids[:, None] == jnp.arange(num_experts)[None, :]).astype(F32)
    gate_prob = jnp.sum(router_probs * expert_onehot, axis=-1)
    mod_mask = jnp.stack([modality == 0, modality == 1]).astype(F32)
    entropy = -jnp.sum(router_probs * log_probs, axis=-1)
    local_stats = jnp.concatenate([jnp.dot(mod_mask, router_probs), jnp.dot(mod_mask, entropy)[:, None], jnp.sum(mod_mask, axis=1, keepdims=True)], axis=1)
    return log_probs, router_probs, expert_onehot, gate_prob, mod_mask, local_stats


def aux_from_stats(stats, num_experts):
    mod_count = stats[:, num_experts + 1]
    mean_probs = stats[:, :num_experts] / mod_count[:, None]
    aux_loss = jnp.sum(stats[:, num_experts] / mod_count) + jnp.sum(mean_probs * jnp.log(mean_probs))
    return aux_loss, mean_probs, mod_count


def router_backward(x_loc, router, log_probs, router_probs, expert_onehot, mod_mask, mean_probs, mod_count, d_gate):
    inv_count = jnp.dot(1.0 / mod_count, mod_mask)
    global_part = jnp.einsum("mt,me->te", mod_mask, jnp.log(mean_probs) / mod_count[:, None])
    d_probs = expert_onehot * d_gate[:, None] + global_part - log_probs * inv_count[:, None]
    d_logits = router_probs * (d_probs - jnp.sum(d_probs * router_probs, axis=-1, keepdims=True))
    d_router_part = jnp.einsum("tw,te->we", x_loc, d_logits, precision=lax.Precision.HIGHEST, preferred_element_type=F32)
    dx_router = jnp.einsum("te,we->tw", d_logits, router, precision=lax.Precision.HIGHEST, preferred_element_type=F32)
    return d_router_part, dx_router.astype(BF16)


def solution(mesh):
    token_spec = P(ALL_AXES)
    expert_spec = P("ep")
    swap = [(i, 1 - i) for i in range(2)]

    def local_step(x_loc, modality, router, expert_ids, priority, w_in, b_in, w_out, b_out, dy_loc):
        num_tokens, width = x_loc.shape
        num_experts = router.shape[1]
        capacity = num_tokens // num_experts
        half = num_experts // 2
        mine = lax.axis_index("dp")
        order = jnp.argsort(expert_ids * num_tokens + priority)
        counts = jnp.sum((expert_ids[:, None] == jnp.arange(num_experts)[None, :]).astype(jnp.int32), axis=0)
        starts = jnp.cumsum(counts) - counts
        x_slots, d_slots = slot_tables(order, starts, counts, capacity)

        def to_owner(table, slots):
            rows = jnp.take(table, slots, axis=0, mode="clip").reshape(half, capacity, width)
            return lax.all_to_all(rows, "ep", 0, 0, tiled=True)

        def pick(table, slots):
            return jnp.take(table, slots, axis=0, mode="clip").reshape(half, capacity, width)

        def swap_rows(rows):
            return lax.all_to_all(rows, "ep", 0, 0, tiled=True)

        x_other = swap_rows(pick(x_loc, x_slots[0]))
        log_probs, router_probs, expert_onehot, gate_prob, mod_mask, local_stats = router_forward(x_loc, modality, router, expert_ids)
        dy_f32 = dy_loc.astype(F32)
        d_tok = jnp.pad((gate_prob[:, None] * dy_f32).astype(BF16), ((0, 8), (0, 0)))
        d_other = swap_rows(pick(d_tok, d_slots[0]))
        x_send = pick(x_loc, x_slots[1])
        d_send = pick(d_tok, d_slots[1])
        stats_block = jnp.pad(local_stats, ((0, 6), (0, 128 - num_experts - 2)))
        y_mine, dx_mine, g_in, g_out, gb_in, gb_out, stats_sum = exchange_call(mesh, x_send, d_send, x_other, d_other, w_in, b_in, w_out, b_out, stats_block)
        aux_loss, mean_probs, mod_count = aux_from_stats(stats_sum[:2, :num_experts + 2], num_experts)
        sel_other = jnp.reshape(1 - mine, (1,)).astype(jnp.int32)
        sel_other, _ = lax.optimization_barrier((sel_other, stats_sum))
        g_bias = jnp.concatenate([gb_in, gb_out], axis=1).astype(BF16)
        far_out = lax.ppermute(g_out, "dp", swap)
        far_in = lax.ppermute(g_in, "dp", swap)
        far_bias = lax.ppermute(g_bias, "dp", swap)
        y_other, dx_other = expert_call(sel_other, x_other, d_other, w_in, b_in, w_out, b_out)
        y_back = [r.reshape(half * capacity, width) for r in (swap_rows(y_other), y_mine)]
        dx_back = [r.reshape(half * capacity, width) for r in (swap_rows(dx_other), dx_mine)]

        def both(near, far):
            first = mine == 0
            return jnp.stack([jnp.where(first, near, far), jnp.where(first, far, near)])

        rank = jnp.argsort(order)
        ids = jnp.arange(num_experts)
        position = rank - jnp.sum(jnp.where(expert_ids[:, None] == ids[None, :], starts[None, :], 0), axis=1)
        keep_mask = position < capacity
        place = jnp.where(lax.rem(expert_ids, 2) == mine, half, 0) + expert_ids // 2
        token_slot = place * capacity + jnp.minimum(position, capacity - 1)
        keep_col = keep_mask[:, None]

        y_tok = jnp.take(jnp.concatenate(y_back), token_slot, axis=0, mode="clip").astype(F32)
        out_tokens = jnp.where(keep_col, gate_prob[:, None] * y_tok, 0.0).astype(BF16)
        d_gate = jnp.where(keep_mask, jnp.sum(dy_f32 * y_tok, axis=-1), 0.0)
        d_router_part, dx_router = router_backward(x_loc, router, log_probs, router_probs, expert_onehot, mod_mask, mean_probs, mod_count, d_gate)
        dx_router = lax.optimization_barrier(dx_router)
        dx_expert = jnp.where(keep_col, jnp.take(jnp.concatenate(dx_back), token_slot, axis=0, mode="clip"), 0).astype(BF16)
        dx_tokens, d_router_part = lax.optimization_barrier((dx_expert + dx_router, d_router_part))
        d_router = device_sum(d_router_part.T.reshape(-1, 128), mesh, 2).reshape(num_experts, width).T
        bias = both(g_bias[0], far_bias[0])
        hidden = w_in.shape[-1]
        return (out_tokens, aux_loss, dx_tokens, d_router, both(g_in, far_in), bias[:, :hidden], both(g_out, far_out), bias[:, hidden:])

    return jax.shard_map(
        local_step,
        mesh=mesh,
        in_specs=(token_spec, token_spec, P(), token_spec, token_spec, expert_spec, expert_spec, expert_spec, expert_spec, token_spec),
        out_specs=(token_spec, P(), token_spec, P(), expert_spec, expert_spec, expert_spec, expert_spec),
        check_vma=False,
    )
```

time: 2210 us -> 984 us (0.45)
  blocking collectives: 1160 us -> 0 us
  Pallas kernels: 0 us -> 439 us
  matrix products: 419 us -> 44.2 us
  local copies, waits for them, and re-layouts: 378 us -> 200 us
  other arithmetic: 82.5 us -> 113 us
  starting transfers between devices: 22.3 us -> 45.7 us
    psum x3 -> x0, blocking collectives: 1160 us -> none  [the longest x1 858 us: local_step(): expert_grads = lax.psum((d_w_in, d_b_in, d_w_out, d_b_out), 'dp')]
    pallas_call x0 -> x4, Pallas kernels: none -> 439 us  [the longest x1 323 us: exchange_call(): pl.pallas_call(functools.partial(exchange_body, ep_size, count, fchunk),...]
    dot_general x6 -> x0, matrix products: 372 us -> none  [the longest x1 106 us: local_step(): jnp.einsum('ecw,efw->ecf', d_recv, w_out, preferred_element_type=jnp.floa...]
    convert_element_type x2 -> x0, local copies, waits for them, and re-layouts: 113 us -> none  [the longest x1 88.8 us: local_step(): expert_out.astype(jnp.bfloat16)]
    all_to_all x4, waiting for transfers between devices: 140 us -> 64.6 us  [swap_rows(): return lax.all_to_all(rows, 'ep', 0, 0, tiled=True)]
    ppermute x0 -> x3, waiting for transfers between devices: none -> 64.6 us  [the longest x1 64.5 us: local_step(): far_bias = lax.ppermute(g_bias, 'dp', swap)]
    all_to_all x4 -> x0, local copies, waits for them, and re-layouts: 44.7 us -> none  [the longest x1 11.9 us: local_step(): d_back = lax.all_to_all(d_rows, 'ep', 1, 0, tiled=True)]
    another operation x2 -> x10, other arithmetic: 0.16 us -> 34.4 us  [the longest x6 34.2 us: both(): return jnp.stack([jnp.where(first, near, far), jnp.where(first, far, near)])]
  transfers between devices with their start and end apart: 4 -> 7, of which waited for: 1 -> 3; matrix products, arithmetic and copies ran while one was open for 2% -> 22% of each run, Pallas kernels for 0% -> 10%
where the time goes in v1:
time: 984 us; the launch traced here: 975 us
  Pallas kernels  439 us (45%)
  local copies, waits for them, and re-layouts  200 us (20%)
  waiting for transfers between devices  129 us (13%)
  other arithmetic  113 us (11%)
  starting transfers between devices  45.7 us (5%)
  matrix products  44.2 us (4%)
    pallas_call x1, Pallas kernels, exchange_call(): pl.pallas_call(functools.partial(exchange_body, ep_size, count, fchunk),...  323 us
    gather x4, local copies, waits for them, and re-layouts, pick(): jnp.take(table, slots, axis=0, mode='clip').reshape(half, capacity, width)  101 us
    pallas_call x1, Pallas kernels, expert_call(): pl.pallas_call(body, grid_spec=pltpu.PrefetchScalarGridSpec(num_scalar_pr...  97.8 us
    all_to_all x4, waiting for transfers between devices, swap_rows(): return lax.all_to_all(rows, 'ep', 0, 0, tiled=True)  64.6 us
    ppermute x1, waiting for transfers between devices, local_step(): far_bias = lax.ppermute(g_bias, 'dp', swap)  64.5 us
    gather x1, local copies, waits for them, and re-layouts, local_step(): jnp.take(jnp.concatenate(dx_back), token_slot, axis=0, mode='clip')  43.3 us
    gather x1, local copies, waits for them, and re-layouts, local_step(): jnp.take(jnp.concatenate(y_back), token_slot, axis=0, mode='clip')  43.2 us
    all_to_all x4, starting transfers between devices, swap_rows(): return lax.all_to_all(rows, 'ep', 0, 0, tiled=True)  43.1 us
  transfers between devices with their start and end apart: 7, of which 3 were waited for; matrix products, arithmetic and copies ran while one was open for 22% of the time, Pallas kernels for 10%

profile of v1, /device:TPU:0, one launch (start us, length us, event | category | flops | bytes accessed | tf_op | source)
XLA Modules:
  0.0 975.3 jit_solution(10139051361668101934)
XLA Ops:
  1.4 12.8 %fusion.21 = (f32[8192]{0:T(1024)S(1)}, f32[8192,16]{0,1:T(8,128)S(1)}) fusion(bf16[8192,768]{1,0:T(8,128)(2,1)} %param.10, f32[768,16]{0,1:T(8,128)S(1)} %copy-done), kind=kOutput, calls=%fused_computation.87 | convolution fusion | flops 1208082432 | bytes 13189120 | tf_op jit(solution)/shard_map/dot_general | solution.py:493
  16.3 6.8 sort.31
  23.7 7.6 fusion
  31.3 5.1 pad.13
  38.7 25.3 %gather_fusion.3 = bf16[4096,768]{1,0:T(8,128)(2,1)} fusion(bf16[8200,768]{1,0:T(8,128)(2,1)} %pad.13, s32[4096]{0:T(1024)S(1)} %get-tuple-element.54), kind=kCustom, calls=%fused_computation.3 | custom fusion | bytes 12599296 | tf_op jit(solution)/shard_map/jit(_take)/gather | solution.py:542
  64.0 5.8 all-to-all-start.1
  69.8 25.3 %gather_fusion.2 = bf16[4096,768]{1,0:T(8,128)(2,1)} fusion(bf16[8192,768]{1,0:T(8,128)(2,1)} %param.10, s32[4096]{0:T(1024)S(1)} %get-tuple-element.65), kind=kCustom, calls=%fused_computation.2 | custom fusion | bytes 12599296 | tf_op jit(solution)/shard_map/jit(_take)/gather | solution.py:542
  95.0 46.4 %all-to-all-done.1.do.refs_2_ = bf16[8,512,768]{2,1,0:T(8,128)(2,1)} async-done(((bf16[8,512,768]{2,1,0:T(8,128)(2,1)}), bf16[8,512,768]{2,1,0:T(8,128)(2,1)}, u32[]{:S(2)}, u32[]{:S(2)}) %all-to-all-start.1) | async-done | bytes 6291488 | tf_op jit(solution)/shard_map/all_to_all | solution.py:545
  141.5 4.8 all-to-all-start
  146.7 25.3 %gather_fusion.1 = bf16[4096,768]{1,0:T(8,128)(2,1)} fusion(bf16[8200,768]{1,0:T(8,128)(2,1)} %pad.13, s32[4096]{0:T(1024)S(1)} %get-tuple-element.55), kind=kCustom, calls=%fused_computation.1 | custom fusion | bytes 12599296 | tf_op jit(solution)/shard_map/jit(_take)/gather | solution.py:542
  172.0 25.3 %gather_fusion = bf16[4096,768]{1,0:T(8,128)(2,1)} fusion(bf16[8192,768]{1,0:T(8,128)(2,1)} %param.10, s32[4096]{0:T(1024)S(1)} %get-tuple-element.64), kind=kCustom, calls=%fused_computation | custom fusion | bytes 12599296 | tf_op jit(solution)/shard_map/jit(_take)/gather | solution.py:542
  199.6 18.1 %all-to-all-done.xo.refs_1_ = bf16[8,512,768]{2,1,0:T(8,128)(2,1)} async-done(((bf16[8,512,768]{2,1,0:T(8,128)(2,1)}), bf16[8,512,768]{2,1,0:T(8,128)(2,1)}, u32[]{:S(2)}, u32[]{:S(2)}) %all-to-all-start) | async-done | bytes 6291488 | tf_op jit(solution)/shard_map/all_to_all | solution.py:545
  217.7 322.7 %exchange.1 = (bf16[8,512,768]{2,1,0:T(8,128)(2,1)}, bf16[8,512,768]{2,1,0:T(8,128)(2,1)}, bf16[768,3072]{1,0:T(8,128)(2,1)}, bf16[3072,768]{1,0:T(8,128)(2,1)},...) custom-call(bf16[8,512,768]{2,1,0:T(8,128)(2,1)} %bitcast.58, ...), custom_call_target="tpu_custom_call" | custom-call | flops 193273528320 | bytes 50331648 | tf_op jit(solution)/shard_map/exchange/pallas_call | solution.py:479
  542.5 97.8 %expert_rows.1 = (bf16[8,512,768]{2,1,0:T(8,128)(2,1)}, bf16[8,512,768]{2,1,0:T(8,128)(2,1)}) custom-call(s32[1]{0:T(128)} %bitcast.1.refs_0_, bf16[8,512,768]{2,1,0:T(8,128)(2,1)} %all-to-all-done.xo.refs_1_, bf16[8,512,768]{2,1,0:T(8,128)(2,1)} %all-to-all-done.1.do.refs_2_, bf16[2,768,3072]{2,1,0:T(8,128)(2,1)} %refs_3_.1, ...), custom_call_target="tpu_custom_call" | custom-call | flops 77309411328 | bytes 25165824 | tf_op jit(solution)/shard_map/expert_rows/pallas_call | solution.py:159
  640.4 16.5 %all-to-all-start.2 = ((bf16[8,512,768]{2,1,0:T(8,128)(2,1)}), bf16[8,512,768]{2,1,0:T(8,128)(2,1)}, u32[]{:S(2)}, u32[]{:S(2)}) async-start(bf16[8,512,768]{2,1,0:T(8,128)(2,1)} %get-tuple-element.30), calls=%async_computation.2 | async-start | bytes 12582912 | tf_op jit(solution)/shard_map/all_to_all | solution.py:545
  657.1 6.8 sort.32
  667.5 64.5 %collective-permute-done.1 = bf16[1,3840]{1,0:T(2,128)(2,1)S(1)} collective-permute-done((bf16[1,3840]{1,0:T(2,128)(2,1)S(1)}, bf16[1,3840]{1,0:T(2,128)(2,1)S(1)}, u32[]{:S(2)}, u32[]{:S(2)}) %collective-permute-start.1) | collective-permute-done | bytes 7712 | tf_op jit(solution)/shard_map/ppermute | solution.py:562
  733.3 8.1 select_bitcast_fusion.1
  741.5 8.4 pad_maximum_fusion.3
  749.8 8.1 select_bitcast_fusion.3
  758.0 16.0 %all-to-all-start.3 = ((bf16[8,512,768]{2,1,0:T(8,128)(2,1)}), bf16[8,512,768]{2,1,0:T(8,128)(2,1)}, u32[]{:S(2)}, u32[]{:S(2)}) async-start(bf16[8,512,768]{2,1,0:T(8,128)(2,1)} %get-tuple-element.32), calls=%async_computation.3 | async-start | bytes 12582912 | tf_op jit(solution)/shard_map/all_to_all | solution.py:545
  774.0 8.4 pad_maximum_fusion.2
  782.4 10.4 %pad_maximum_fusion = bf16[8192,768]{1,0:T(8,128)(2,1)} fusion(bf16[4096,768]{1,0:T(8,128)(2,1)} %bitcast.56, bf16[4096,768]{1,0:T(8,128)(2,1)} %bitcast.17), kind=kLoop, calls=%fused_computation.14 | loop fusion | flops 25165824 | bytes 25165824 | tf_op jit(solution)/shard_map/concatenate | solution.py:579
  792.8 43.2 %gather_fusion.4 = bf16[8192,768]{1,0:T(8,128)(2,1)} fusion(bf16[8192,768]{1,0:T(8,128)(2,1)} %pad_maximum_fusion, s32[8192]{0:T(1024)S(1)} %fusion.13), kind=kCustom, calls=%fused_computation.4 | custom fusion | bytes 25198592 | tf_op jit(solution)/shard_map/jit(_take)/gather | solution.py:579
  836.0 10.4 %fusion.3 = f32[8192]{0:T(1024)S(1)} fusion(bf16[8192,768]{1,0:T(8,128)(2,1)} %gather_fusion.4, bf16[8192,768]{1,0:T(8,128)(2,1)} %param.19), kind=kLoop, calls=%fused_computation.12 | loop fusion | flops 25157632 | bytes 25198592 | tf_op jit(solution)/shard_map/reduce_sum | solution.py:581
  846.9 8.0 convolution_bitcast_fusion
  854.9 22.3 %convolution_convert_fusion = bf16[8192,768]{1,0:T(8,128)(2,1)} fusion(f32[768,16]{0,1:T(8,128)S(1)} %copy-done, f32[8192,16]{0,1:T(8,128)S(1)} %get-tuple-element.63, f32[8192]{0:T(1024)S(1)} %get-tuple-element.62, f32[8192,16]{0,1:T(8,128)S(1)} %copy-done.4, f32[8192]{0:T(1024)S(1)} %copy-done.8, f32[8192]{0:T(1024)S(1)} %copy-done.6), kind=kOutput, calls=%fused_computation.13 | convolution fusion | flops 1214775296 | bytes 13778944 | tf_op jit(solution)/shard_map/te,we->tw/dot_general | solution.py:517
  877.3 10.9 %pad_maximum_fusion.1 = bf16[8192,768]{1,0:T(8,128)(2,1)} fusion(bf16[4096,768]{1,0:T(8,128)(2,1)} %bitcast.55, bf16[4096,768]{1,0:T(8,128)(2,1)} %bitcast.19), kind=kLoop, calls=%fused_computation.15 | loop fusion | flops 25165824 | bytes 25165824 | tf_op jit(solution)/shard_map/concatenate | solution.py:584
  888.1 43.3 %gather_fusion.5 = bf16[8192,768]{1,0:T(8,128)(2,1)} fusion(bf16[8192,768]{1,0:T(8,128)(2,1)} %pad_maximum_fusion.1, s32[8192]{0:T(1024)S(1)} %fusion.13), kind=kCustom, calls=%fused_computation.5 | custom fusion | bytes 25198592 | tf_op jit(solution)/shard_map/jit(_take)/gather | solution.py:584
  931.4 14.7 %fusion.2 = bf16[8192,768]{1,0:T(8,128)(2,1)} fusion(bf16[8192,768]{1,0:T(8,128)(2,1)} %gather_fusion.4, f32[8192]{0:T(1024)S(1)} %copy-done.12, pred[8192]{0:T(1024)(128)(4,1)S(1)} %get-tuple-element.45), kind=kLoop, calls=%fused_computation.11 | loop fusion | flops 25165824 | bytes 25206784 | tf_op jit(solution)/shard_map/convert_element_type | solution.py:580
  947.9 6.8 select_add_fusion
  955.3 17.1 %device_sum.1 = f32[96,128]{1,0:T(8,128)} custom-call(f32[96,128]{1,0:T(8,128)} %reshape.148.x_ref), custom_call_target="tpu_custom_call" | custom-call | flops 10000000 | bytes 1000000 | tf_op jit(solution)/shard_map/device_sum/pallas_call | solution.py:240
  (101 shorter events, 18.7 us)
Async XLA Ops:
  0.6 0.8 copy-start
  0.6 13.8 %copy-start.9 = (s32[8192]{0:T(1024)S(1)}, s32[8192]{0:T(1024)}, u32[]{:S(2)}) copy-start(s32[8192]{0:T(1024)} %param.13) | copy-start | bytes 98308
  0.7 15.6 %copy-start.15 = (s32[8192]{0:T(1024)S(1)}, s32[8192]{0:T(1024)}, u32[]{:S(2)}) copy-start(s32[8192]{0:T(1024)} %param.14) | copy-start | bytes 98308
  14.2 184.4 %copy-start.3 = (f32[8192,16]{0,1:T(8,128)}, f32[8192,16]{0,1:T(8,128)S(1)}, u32[]{:S(2)}) copy-start(f32[8192,16]{0,1:T(8,128)S(1)} %get-tuple-element.61) | copy-start | bytes 1572868
  14.2 184.4 %copy-start.5 = (f32[8192]{0:T(1024)}, f32[8192]{0:T(1024)S(1)}, u32[]{:S(2)}) copy-start(f32[8192]{0:T(1024)S(1)} %get-tuple-element.60) | copy-start | bytes 98308
  14.4 184.2 %copy-start.7 = (f32[8192]{0:T(1024)}, f32[8192]{0:T(1024)S(1)}, u32[]{:S(2)}) copy-start(f32[8192]{0:T(1024)S(1)} %log.13) | copy-start | bytes 98308
  14.9 16.4 %copy-start.11 = (f32[8192]{0:T(1024)}, f32[8192]{0:T(1024)S(1)}, u32[]{:S(2)}) copy-start(f32[8192]{0:T(1024)S(1)} %get-tuple-element.41) | copy-start | bytes 98308
  23.0 8.2 copy-start.13
  64.0 77.5 %all-to-all-start.1 = ((bf16[8,512,768]{2,1,0:T(8,128)(2,1)}), bf16[8,512,768]{2,1,0:T(8,128)(2,1)}, u32[]{:S(2)}, u32[]{:S(2)}) async-start(bf16[8,512,768]{2,1,0:T(8,128)(2,1)} %bitcast.54), calls=%async_computation.1 | async-start | bytes 12582912 | tf_op jit(solution)/shard_map/all_to_all | solution.py:545
  95.0 51.2 %copy-start.18 = (s32[8192]{0:T(1024)S(1)}, s32[8192]{0:T(1024)}, u32[]{:S(2)}) copy-start(s32[8192]{0:T(1024)} %param.11) | copy-start | bytes 98308
  141.5 76.3 %all-to-all-start = ((bf16[8,512,768]{2,1,0:T(8,128)(2,1)}), bf16[8,512,768]{2,1,0:T(8,128)(2,1)}, u32[]{:S(2)}, u32[]{:S(2)}) async-start(bf16[8,512,768]{2,1,0:T(8,128)(2,1)} %bitcast.53), calls=%async_computation | async-start | bytes 12582912 | tf_op jit(solution)/shard_map/all_to_all | solution.py:545
  146.6 52.1 %copy-start.16 = (pred[2,8192]{1,0:T(4,128)(4,1)}, pred[2,8192]{1,0:T(4,128)(4,1)S(1)}, u32[]{:S(2)}) copy-start(pred[2,8192]{1,0:T(4,128)(4,1)S(1)} %get-tuple-element.47) | copy-start | bytes 49156
  172.0 25.3 %copy-start.20 = (bf16[2,3072]{1,0:T(2,128)(2,1)S(1)}, bf16[2,3072]{1,0:T(2,128)(2,1)}, u32[]{:S(2)}) copy-start(bf16[2,3072]{1,0:T(2,128)(2,1)} %param.16) | copy-start | bytes 36868
  172.0 25.9 %copy-start.22 = (bf16[2,768]{1,0:T(2,128)(2,1)S(1)}, bf16[2,768]{1,0:T(2,128)(2,1)}, u32[]{:S(2)}) copy-start(bf16[2,768]{1,0:T(2,128)(2,1)} %param.18) | copy-start | bytes 9220
  540.4 192.9 %collective-permute-start.2 = (bf16[3072,768]{1,0:T(8,128)(2,1)}, bf16[3072,768]{1,0:T(8,128)(2,1)}, u32[]{:S(2)}, u32[]{:S(2)}) collective-permute-start(bf16[3072,768]{1,0:T(8,128)(2,1)} %get-tuple-element.39), channel_id=1, source_target_pairs={{0,8},{8,0},{1,9},{9,1},{2,10},{10,2},{3,11},{11,3},{4,12},{12,4},... | collective-permute-start | bytes 14155784 | tf_op jit(solution)/shard_map/ppermute | solution.py:560
  541.0 208.8 %collective-permute-start = (bf16[768,3072]{1,0:T(8,128)(2,1)}, bf16[768,3072]{1,0:T(8,128)(2,1)}, u32[]{:S(2)}, u32[]{:S(2)}) collective-permute-start(bf16[768,3072]{1,0:T(8,128)(2,1)} %get-tuple-element.36), channel_id=1, source_target_pairs={{0,8},{8,0},{1,9},{9,1},{2,10},{10,2},{3,11},{11,3},{4,12},{12,4},... | collective-permute-start | bytes 14155784 | tf_op jit(solution)/shard_map/ppermute | solution.py:561
  640.3 16.5 %copy-start.10 = (s32[8192]{0:T(1024)S(1)}, s32[8192]{0:T(1024)}, u32[]{:S(2)}) copy-start(s32[8192]{0:T(1024)} %param.13) | copy-start | bytes 98308
  640.3 16.5 %copy-start.25 = (s32[16]{0:T(128)S(1)}, s32[16]{0:T(128)}, u32[]{:S(2)}) copy-start(s32[16]{0:T(128)} %copy-done.24) | copy-start | bytes 196
  640.3 16.7 %copy-start.14 = (s32[8192]{0:T(1024)S(1)}, s32[8192]{0:T(1024)}, u32[]{:S(2)}) copy-start(s32[8192]{0:T(1024)} %copy-done.13) | copy-start | bytes 98308
  640.3 23.5 %copy-start.19 = (f32[1,3072]{1,0:T(1,128)S(1)}, f32[1,3072]{1,0:T(1,128)}, u32[]{:S(2)}) copy-start(f32[1,3072]{1,0:T(1,128)} %get-tuple-element.37) | copy-start | bytes 36868
  640.3 23.6 %copy-start.21 = (f32[1,768]{1,0:T(1,128)S(1)}, f32[1,768]{1,0:T(1,128)}, u32[]{:S(2)}) copy-start(f32[1,768]{1,0:T(1,128)} %get-tuple-element.38) | copy-start | bytes 9220
  640.4 24.2 %copy-start.23 = (f32[8,128]{1,0:T(8,128)S(1)}, f32[8,128]{1,0:T(8,128)}, u32[]{:S(2)}) copy-start(f32[8,128]{1,0:T(8,128)} %get-tuple-element.28) | copy-start | bytes 12292
  640.4 25.1 %copy-start.17 = (pred[2,8192]{1,0:T(4,128)(4,1)S(1)}, pred[2,8192]{1,0:T(4,128)(4,1)}, u32[]{:S(2)}) copy-start(pred[2,8192]{1,0:T(4,128)(4,1)} %copy-done.16) | copy-start | bytes 49156
  640.4 117.6 %all-to-all-start.2 = ((bf16[8,512,768]{2,1,0:T(8,128)(2,1)}), bf16[8,512,768]{2,1,0:T(8,128)(2,1)}, u32[]{:S(2)}, u32[]{:S(2)}) async-start(bf16[8,512,768]{2,1,0:T(8,128)(2,1)} %get-tuple-element.30), calls=%async_computation.2 | async-start | bytes 12582912 | tf_op jit(solution)/shard_map/all_to_all | solution.py:545
  664.0 68.1 %collective-permute-start.1 = (bf16[1,3840]{1,0:T(2,128)(2,1)S(1)}, bf16[1,3840]{1,0:T(2,128)(2,1)S(1)}, u32[]{:S(2)}, u32[]{:S(2)}) collective-permute-start(bf16[1,3840]{1,0:T(2,128)(2,1)S(1)} %pad_maximum_fusion.4), channel_id=1, source_target_pairs={{0,8},{8,0},{1,9},{9,1},{2,10},{10,2},{3,11},{11,3},{4,12},{12,4},... | collective-permute-start | bytes 23048 | tf_op jit(solution)/shard_map/ppermute | solution.py:562
  758.0 119.3 %all-to-all-start.3 = ((bf16[8,512,768]{2,1,0:T(8,128)(2,1)}), bf16[8,512,768]{2,1,0:T(8,128)(2,1)}, u32[]{:S(2)}, u32[]{:S(2)}) async-start(bf16[8,512,768]{2,1,0:T(8,128)(2,1)} %get-tuple-element.32), calls=%async_computation.3 | async-start | bytes 12582912 | tf_op jit(solution)/shard_map/all_to_all | solution.py:545
  836.0 10.4 %copy-start.4 = (f32[8192,16]{0,1:T(8,128)S(1)}, f32[8192,16]{0,1:T(8,128)}, u32[]{:S(2)}) copy-start(f32[8192,16]{0,1:T(8,128)} %copy-done.3) | copy-start | bytes 1572868
  836.0 10.4 %copy-start.6 = (f32[8192]{0:T(1024)S(1)}, f32[8192]{0:T(1024)}, u32[]{:S(2)}) copy-start(f32[8192]{0:T(1024)} %copy-done.5) | copy-start | bytes 98308
  836.0 10.4 %copy-start.8 = (f32[8192]{0:T(1024)S(1)}, f32[8192]{0:T(1024)}, u32[]{:S(2)}) copy-start(f32[8192]{0:T(1024)} %copy-done.7) | copy-start | bytes 98308
  888.1 43.3 %copy-start.12 = (f32[8192]{0:T(1024)S(1)}, f32[8192]{0:T(1024)}, u32[]{:S(2)}) copy-start(f32[8192]{0:T(1024)} %copy-done.11) | copy-start | bytes 98308
  931.4 14.7 %copy-start.1 = (bf16[8192,768]{1,0:T(8,128)(2,1)S(1)}, bf16[8192,768]{1,0:T(8,128)(2,1)}, u32[]{:S(2)}) copy-start(bf16[8192,768]{1,0:T(8,128)(2,1)} %convolution_convert_fusion) | copy-start | bytes 37748740
  931.4 16.5 %copy-start.2 = (bf16[8192,768]{1,0:T(8,128)(2,1)S(1)}, bf16[8192,768]{1,0:T(8,128)(2,1)}, u32[]{:S(2)}) copy-start(bf16[8192,768]{1,0:T(8,128)(2,1)} %gather_fusion.5) | copy-start | bytes 37748740
  (1 other events, 0.5 us)

commit v2 on v0

v2 whole, which is shorter than its diff:
```python
import functools
import jax
import jax.numpy as jnp
from jax import lax
from jax.experimental import pallas as pl
from jax.experimental.pallas import tpu as pltpu
from jax.sharding import PartitionSpec as P

F32 = jnp.float32
BF16 = jnp.bfloat16
VMEM_CAP = 66_000_000
GELU_SCALE = 0.7978845608028654
GELU_CUBE = 0.044715
FCHUNK = 768


def gelu_and_slope(a):
    sq = a * a
    t = jnp.tanh(GELU_SCALE * (a + GELU_CUBE * (a * sq)))
    cdf = 0.5 * (1.0 + t)
    slope = cdf + (0.5 * a) * ((1.0 - t * t) * (GELU_SCALE * (1.0 + (3.0 * GELU_CUBE) * sq)))
    return a * cdf, slope


ALL_AXES = ("dp", "ep")
MESH_ID = pl.DeviceIdType.MESH


def slots_kernel(num_tokens, capacity, scal_ref, order_ref, xs_ref, ds_ref):
    mine = lax.axis_index("dp")
    experts = xs_ref.shape[0] * 128 // capacity
    rows = capacity // 128
    lane = lax.broadcasted_iota(jnp.int32, (rows, 128), 1)
    rank = lax.broadcasted_iota(jnp.int32, (rows, 128), 0) * 128 + lane
    for j in range(experts):
        owner = (1 - mine) if j < experts // 2 else mine
        e = 2 * (j % (experts // 2)) + owner
        start = scal_ref[e]
        count = scal_ref[experts + e]
        block = order_ref[pl.ds(start // 128, 8), :]
        off = lax.rem(start, 128)
        turned = pltpu.roll(block, lax.rem(128 - off, 128), 1)
        tok = jnp.where(lane < 128 - off, turned[:rows], turned[1:rows + 1])
        xs_ref[rows * j:rows * (j + 1), :] = jnp.where(rank < count, tok, 0)
        ds_ref[rows * j:rows * (j + 1), :] = jnp.where(rank < count, tok, num_tokens)


def slot_tables(order, starts, counts, capacity):
    num_tokens = order.shape[0]
    experts = starts.shape[0]
    padded = jnp.pad(order, (0, 1024)).reshape(-1, 128)
    shape = jax.ShapeDtypeStruct((experts * capacity // 128, 128), jnp.int32)
    xs, ds = pl.pallas_call(
        functools.partial(slots_kernel, num_tokens, capacity),
        in_specs=[pl.BlockSpec(memory_space=pltpu.SMEM), pl.BlockSpec(memory_space=pltpu.VMEM)],
        out_specs=[pl.BlockSpec(memory_space=pltpu.VMEM)] * 2,
        out_shape=[shape, shape],
        cost_estimate=pl.CostEstimate(flops=1_000_000, bytes_accessed=200_000, transcendentals=0),
        name="slots",
    )(jnp.concatenate([starts, counts]), padded)
    return xs.reshape(-1), ds.reshape(-1)


def sum_kernel(ep_size, count, x_ref, out_ref, slots, send_sem, recv_sem):
    dp_me, ep_me = lax.axis_index("dp"), lax.axis_index("ep")
    me = dp_me * ep_size + ep_me

    def peer(k):
        p = lax.rem(me + k, count)
        return (p // ep_size, lax.rem(p, ep_size))

    barrier = pltpu.get_barrier_semaphore()
    for k in range(1, count):
        pl.semaphore_signal(barrier, inc=1, device_id=peer(k), device_id_type=MESH_ID)
    pl.semaphore_wait(barrier, count - 1)
    copies = []
    for k in range(1, count):
        c = pltpu.make_async_remote_copy(
            src_ref=x_ref, dst_ref=slots.at[me], send_sem=send_sem.at[k], recv_sem=recv_sem.at[k],
            device_id=peer(k), device_id_type=MESH_ID)
        c.start()
        copies.append(c)
    slots[me] = x_ref[...]
    for c in copies:
        c.wait()
    total = slots[0]
    for k in range(1, count):
        total = total + slots[k]
    out_ref[...] = total


def device_sum(x, mesh, collective_id):
    count = mesh.shape["dp"] * mesh.shape["ep"]
    return pl.pallas_call(
        functools.partial(sum_kernel, mesh.shape["ep"], count),
        in_specs=[pl.BlockSpec(memory_space=pltpu.VMEM)],
        out_specs=pl.BlockSpec(memory_space=pltpu.VMEM),
        out_shape=jax.ShapeDtypeStruct(x.shape, F32),
        scratch_shapes=[pltpu.VMEM((count,) + x.shape, F32), pltpu.SemaphoreType.DMA((count,)), pltpu.SemaphoreType.DMA((count,))],
        compiler_params=pltpu.CompilerParams(collective_id=collective_id, has_side_effects=True),
        cost_estimate=pl.CostEstimate(flops=10_000_000, bytes_accessed=1_000_000, transcendentals=0),
        name="device_sum",
    )(x)


def take_body(n_tables, n_outs, rows_in, rows_out, chunk, q_ref, *refs):
    tables, results = refs[:n_tables], refs[n_tables:n_tables + n_outs]
    wide, inbuf, outs, outbuf, in_sem, out_sem = refs[n_tables + n_outs:]
    width = inbuf.shape[-1]
    parts = width // 128
    per_table = rows_in // chunk // n_tables

    def load(c):
        t, i = c // per_table, c % per_table
        return pltpu.make_async_copy(tables[t].at[pl.ds(i * chunk, chunk), :], inbuf.at[c % 2], in_sem.at[c % 2])

    load(0).start()
    for c in range(rows_in // chunk):
        if c + 1 < rows_in // chunk:
            load(c + 1).start()
        load(c).wait()

        def widen(g, carry, c=c):
            for u in range(2):
                v = inbuf[c % 2, pl.ds(pl.multiple_of(g * 32 + u * 16, 16), 16), :].astype(F32)
                base = (c * chunk // 8 + g * 4 + u * 2) * 8 * parts
                for hh in range(2):
                    for k in range(parts):
                        wide[pl.ds(pl.multiple_of(base + (hh * parts + k) * 8, 8), 8), :] = v[hh * 8:hh * 8 + 8, k * 128:(k + 1) * 128]
            return carry

        lax.fori_loop(0, chunk // 32, widen, 0)
    wide[rows_in * parts:, :] = jnp.zeros((8 * parts, 128), F32)

    steps = rows_out // chunk // n_outs

    def fill(o, out):
        def store(c, slot):
            return pltpu.make_async_copy(outbuf.at[slot], out.at[pl.ds(c * chunk, chunk), :], out_sem.at[slot])

        def chunk_step(c, carry):
            slot = lax.rem(c, 2)

            def rows(g, carry):
                at = [q_ref[(o * steps + c) * chunk + g * 32 + j] for j in range(32)]
                got = [wide[pl.ds(q, parts, stride=8), :] for q in at]
                for j in range(32):
                    outs[pl.ds((g * 4 + j // 8) * 8 * parts + j % 8, parts, stride=8), :] = got[j]
                return carry

            lax.fori_loop(0, chunk // 32, rows, 0)

            @pl.when(c >= 2)
            def _():
                store(c - 2, slot).wait()

            def narrow(g, carry):
                for u in range(2):
                    base = (g * 4 + u * 2) * 8 * parts
                    v = [jnp.concatenate([outs[pl.ds(pl.multiple_of(base + (hh * parts + k) * 8, 8), 8), :] for hh in range(2)], axis=0) for k in range(parts)]
                    outbuf[slot, pl.ds(pl.multiple_of(g * 32 + u * 16, 16), 16), :] = jnp.concatenate(v, axis=1).astype(BF16)
                return carry

            lax.fori_loop(0, chunk // 32, narrow, 0)
            store(c, slot).start()
            return carry

        lax.fori_loop(0, steps, chunk_step, 0)
        for c in range(steps - 2, steps):
            store(c, c % 2).wait()

    for o, out in enumerate(results):
        fill(o, out)


def take_rows(tables, index, n_outs=1, chunk=512):
    rows_in = sum(t.shape[0] for t in tables)
    width = tables[0].shape[1]
    parts = width // 128
    rows_out = index.shape[0]
    q = (index // 8) * (8 * parts) + index % 8
    anyspec = pl.BlockSpec(memory_space=pl.ANY)
    return pl.pallas_call(
        functools.partial(take_body, len(tables), n_outs, rows_in, rows_out, chunk),
        grid_spec=pltpu.PrefetchScalarGridSpec(
            num_scalar_prefetch=1, grid=(1,), in_specs=[anyspec] * len(tables), out_specs=[anyspec] * n_outs,
            scratch_shapes=[pltpu.VMEM(((rows_in + 8) * parts, 128), F32), pltpu.VMEM((2, chunk, width), BF16),
                            pltpu.VMEM((chunk * parts, 128), F32), pltpu.VMEM((2, chunk, width), BF16),
                            pltpu.SemaphoreType.DMA((2,)), pltpu.SemaphoreType.DMA((2,))]),
        out_shape=[jax.ShapeDtypeStruct((rows_out // n_outs, width), BF16)] * n_outs,
        compiler_params=pltpu.CompilerParams(vmem_limit_bytes=VMEM_CAP),
        cost_estimate=pl.CostEstimate(flops=rows_out * 4096 * 8, bytes_accessed=2 * (rows_in + rows_out) * width, transcendentals=0),
        name="take_rows",
    )(q, *tables)


def join_body(*refs):
    pieces, outs, bufs, sems = refs[:8], refs[8:10], refs[10:12], refs[12:]
    mine = lax.axis_index("dp")
    copies = []
    for i, src in enumerate(pieces):
        kind, part, far = i // 4, (i // 2) % 2, i % 2
        owner = 1 - mine if far else mine
        rows, cols = src.shape
        dst = outs[0].at[owner, :, pl.ds(part * cols, cols)] if kind == 0 else outs[1].at[owner, pl.ds(part * rows, rows), :]
        buf = bufs[kind].at[i % 4]
        copies.append((pltpu.make_async_copy(src, buf, sems[0].at[i]), pltpu.make_async_copy(buf, dst, sems[1].at[i])))
    for c in copies:
        c[0].start()
    for c in copies:
        c[0].wait()
        c[1].start()
    for c in copies:
        c[1].wait()


def join_grads(near1, far1, near2, far2):
    width, part = near1[0].shape
    anyspec = pl.BlockSpec(memory_space=pl.ANY)
    pieces = [near1[0], far1[0], near1[1], far1[1], near2[0], far2[0], near2[1], far2[1]]
    return pl.pallas_call(
        join_body,
        in_specs=[anyspec] * 8,
        out_specs=[anyspec] * 2,
        out_shape=[jax.ShapeDtypeStruct((2, width, 2 * part), BF16), jax.ShapeDtypeStruct((2, 2 * part, width), BF16)],
        scratch_shapes=[pltpu.VMEM((4, width, part), BF16), pltpu.VMEM((4, part, width), BF16),
                        pltpu.SemaphoreType.DMA((8,)), pltpu.SemaphoreType.DMA((8,))],
        compiler_params=pltpu.CompilerParams(vmem_limit_bytes=40_000_000),
        cost_estimate=pl.CostEstimate(flops=10_000_000, bytes_accessed=16 * width * part * 2, transcendentals=0),
        name="join_grads",
    )(*pieces)


def exchange_body(ep_size, count, fchunk,
                  xo, dos, xs, ds, w1_hbm, w2_hbm, b1_ref, b2_ref, st_ref,
                  yb, dxb, dxl, g1a, g2a, g1b, g2b, p1a, p2a, gb1_ref, gb2_ref, st_out, dor, xr, dr, xf, df, yl, yol, dxol,
                  w1, w2, acc1, acc2, xv, dv, xt, dt, yacc, dxacc, ystage, dxstage, stage, slots,
                  st_send, st_recv, do_send, do_recv, x_send, x_recv, d_send, d_recv, xf_send, xf_recv, df_send, df_recv,
                  yo_send, yo_recv, dxo_send, dxo_recv, y_send, y_recv, g1_send, g1_recv, g2_send, g2_recv, w_sem, in_sem, out_sem, g_sem):
    width = w1.shape[0]
    hidden = w1.shape[1]
    mine, e = lax.axis_index("dp"), lax.axis_index("ep")
    me = mine * ep_size + e

    def anyone(k):
        p = lax.rem(me + k, count)
        return (p // ep_size, lax.rem(p, ep_size))

    def dest(k):
        return lax.rem(e + k, ep_size)

    def source(k):
        return lax.rem(e + ep_size - k, ep_size)

    def remote(src, dst, send, recv, dp, ep):
        return pltpu.make_async_remote_copy(src_ref=src, dst_ref=dst, send_sem=send, recv_sem=recv,
                                            device_id=(dp, ep), device_id_type=MESH_ID)

    def stat_copy(k):
        dp, ep = anyone(k)
        return remote(st_ref, slots.at[me], st_send.at[k], st_recv.at[k], dp, ep)

    def out_copy(src, dst, send, recv):
        return lambda k: remote(src.at[dest(k)], dst.at[e], send.at[k], recv.at[k], mine, dest(k))

    def back_copy(src, dst, base, send, recv):
        return lambda k: remote(src.at[source(k)], dst.at[base + e], send.at[k], recv.at[k], mine, source(k))

    do_copy = out_copy(dos, dor, do_send, do_recv)
    x_copy = out_copy(xs, xr, x_send, x_recv)
    d_copy = out_copy(ds, dr, d_send, d_recv)
    yo_copy = back_copy(yol, yb, 0, yo_send, yo_recv)
    dxo_copy = back_copy(dxol, dxb, 0, dxo_send, dxo_recv)
    y_copy = back_copy(yl, yb, ep_size, y_send, y_recv)

    def xf_copy(k):
        return remote(xo.at[source(k)], xf.at[source(k)], xf_send.at[k], xf_recv.at[k], 1 - mine, e)

    def df_copy(k):
        return remote(dor.at[source(k)], df.at[source(k)], df_send.at[k], df_recv.at[k], 1 - mine, e)

    def df_own():
        return remote(dos.at[e], df.at[e], df_send.at[0], df_recv.at[0], 1 - mine, e)

    def start_all(copies):
        for c in copies:
            c.start()

    def wait_all(copies):
        for c in copies:
            c.wait()

    def weights(which):
        return (pltpu.make_async_copy(w1_hbm.at[which], w1, w_sem.at[0]), pltpu.make_async_copy(w2_hbm.at[which], w2, w_sem.at[1]))

    def fetch(x_src, d_src, slot):
        return (pltpu.make_async_copy(x_src, xv.at[slot], in_sem.at[0, slot]),
                pltpu.make_async_copy(d_src, dv.at[slot], in_sem.at[1, slot]))

    def chunk(j, slot, which, want_rows, want_dw):
        cols = pl.ds(pl.multiple_of(j * fchunk, fchunk), fchunk)
        w1c = w1[:, cols]
        w2c = w2[cols, :]
        a = jnp.dot(xv[slot], w1c, preferred_element_type=F32) + b1_ref[which, :, cols].astype(F32)
        dh = lax.dot_general(dv[slot], w2c, (((1,), (1,)), ((), ())), preferred_element_type=F32)
        h, slope = gelu_and_slope(a)
        da = dh.astype(BF16).astype(F32) * slope
        h16 = h.astype(BF16)
        da16 = da.astype(BF16)
        if want_rows:
            yacc[...] += jnp.dot(h16, w2c, preferred_element_type=F32)
            dxacc[...] += lax.dot_general(da16, w1c, (((1,), (1,)), ((), ())), preferred_element_type=F32)
        if want_dw:
            gb1_ref[:, cols] += jnp.sum(da, axis=0, keepdims=True)
            acc1[:, cols] += jnp.dot(xt[...], da16, preferred_element_type=F32)
            acc2[:, cols] += jnp.dot(dt[...], h16, preferred_element_type=F32)

    def turn(slot):
        xt[...] = xv[slot].T
        dt[...] = dv[slot].T

    def add_bias_grad(slot):
        gb2_ref[...] += jnp.sum(dv[slot].astype(F32), axis=0, keepdims=True)

    def tile(slot, which, want_dw):
        if want_dw:
            turn(slot)
            add_bias_grad(slot)
        yacc[...] = jnp.broadcast_to(b2_ref[which].astype(F32), yacc.shape)
        dxacc[...] = jnp.zeros_like(dxacc)

        def step(j, carry):
            chunk(j, slot, which, True, want_dw)
            return carry

        lax.fori_loop(0, hidden // fchunk, step, 0)

    def put_rows(y_dst, dx_dst):
        return (pltpu.make_async_copy(ystage, y_dst, out_sem.at[0]), pltpu.make_async_copy(dxstage, dx_dst, out_sem.at[1]))

    start_all(weights(1 - mine))
    start_all(fetch(xo.at[e], dos.at[e], 0))
    barrier = pltpu.get_barrier_semaphore()
    for k in range(1, count):
        pl.semaphore_signal(barrier, inc=1, device_id=anyone(k), device_id_type=MESH_ID)
    pl.semaphore_wait(barrier, count - 1)
    for k in range(1, count):
        stat_copy(k).start()
    for k in range(1, ep_size):
        do_copy(k).start()
    df_own().start()
    for k in range(ep_size):
        xf_copy(k).start()
    for k in range(1, ep_size):
        x_copy(k).start()
        d_copy(k).start()
    slots[me] = st_ref[...]
    acc1[...] = jnp.zeros_like(acc1)
    acc2[...] = jnp.zeros_like(acc2)
    gb1_ref[...] = jnp.zeros_like(gb1_ref)
    gb2_ref[...] = jnp.zeros_like(gb2_ref)
    wait_all(weights(1 - mine))

    def other_step(k, carry):
        slot = lax.rem(k, 2)
        src = source(k)
        wait_all(fetch(xo.at[src], dos.at[src], slot))

        @pl.when(k < ep_size - 1)
        def _():
            do_copy(k + 1).wait_recv()
            df_copy(k + 1).start()
            start_all(fetch(xo.at[source(k + 1)], dor.at[source(k + 1)], lax.rem(k + 1, 2)))

        @pl.when(k >= 1)
        def _():
            wait_all(put_rows(yol.at[source(k - 1)], dxol.at[source(k - 1)]))

        @pl.when(k >= 2)
        def _():
            yo_copy(k - 1).start()
            dxo_copy(k - 1).start()

        tile(slot, 1 - mine, False)
        ystage[...] = yacc[...].astype(BF16)
        dxstage[...] = dxacc[...].astype(BF16)

        @pl.when(k == 0)
        def _():
            start_all(put_rows(yb.at[e], dxb.at[e]))

        @pl.when(k > 0)
        def _():
            start_all(put_rows(yol.at[src], dxol.at[src]))

        return carry

    last = ep_size - 1
    lax.fori_loop(0, ep_size, other_step, 0)
    start_all(weights(mine))
    start_all(fetch(xs.at[e], ds.at[e], 0))
    wait_all(put_rows(yol.at[source(last)], dxol.at[source(last)]))
    yo_copy(last).start()
    dxo_copy(last).start()
    wait_all(weights(mine))

    def near_step(k, carry):
        slot = lax.rem(k, 2)
        src = source(k)
        wait_all(fetch(xr.at[src], dr.at[src], slot))

        @pl.when(k < last)
        def _():
            x_copy(k + 1).wait_recv()
            d_copy(k + 1).wait_recv()
            start_all(fetch(xr.at[source(k + 1)], dr.at[source(k + 1)], lax.rem(k + 1, 2)))

        @pl.when(k >= 1)
        def _():
            wait_all(put_rows(yl.at[source(k - 1)], dxl.at[source(k - 1)]))

        @pl.when(k >= 2)
        def _():
            y_copy(k - 1).start()

        tile(slot, mine, True)
        ystage[...] = yacc[...].astype(BF16)
        dxstage[...] = dxacc[...].astype(BF16)

        @pl.when(k == 0)
        def _():
            start_all(put_rows(yb.at[ep_size + e], dxl.at[e]))

        @pl.when(k > 0)
        def _():
            start_all(put_rows(yl.at[src], dxl.at[src]))

        return carry

    lax.fori_loop(0, ep_size, near_step, 0)
    xf_copy(0).wait_recv()
    df_own().wait_recv()
    start_all(fetch(xf.at[e], df.at[e], 0))
    wait_all(put_rows(yl.at[source(last)], dxl.at[source(last)]))
    y_copy(last).start()

    chunks = hidden // fchunk
    early = chunks // 2
    half = early * fchunk

    def cols_of(j):
        return pl.ds(pl.multiple_of(j * fchunk, fchunk), fchunk)

    def grad_copies(j):
        return (remote(g1a.at[:, cols_of(j)], p1a.at[:, cols_of(j)], g1_send.at[j], g1_recv.at[j], 1 - mine, e),
                remote(g2a.at[cols_of(j), :], p2a.at[cols_of(j), :], g2_send.at[j], g2_recv.at[j], 1 - mine, e))

    def grad_out(j, late):
        if late:
            return (pltpu.make_async_copy(stage.at[0], g1b.at[:, cols_of(j - early)], g_sem.at[0]),
                    pltpu.make_async_copy(stage.at[1], g2b.at[cols_of(j - early), :], g_sem.at[1]))
        return (pltpu.make_async_copy(stage.at[0], g1a.at[:, cols_of(j)], g_sem.at[0]),
                pltpu.make_async_copy(stage.at[1], g2a.at[cols_of(j), :], g_sem.at[1]))

    def far_step(n, carry):
        j = n // ep_size
        k = lax.rem(n, ep_size)
        slot = lax.rem(n, 2)
        nxt = lax.rem(k + 1, ep_size)
        wait_all(fetch(xf.at[source(k)], df.at[source(k)], slot))

        @pl.when(n < last)
        def _():
            xf_copy(k + 1).wait_recv()
            df_copy(k + 1).wait_recv()

        @pl.when(n < chunks * ep_size - 1)
        def _():
            start_all(fetch(xf.at[source(nxt)], df.at[source(nxt)], lax.rem(n + 1, 2)))

        @pl.when((k == 1) & (j >= 1) & (j <= early))
        def _():
            wait_all(grad_out(j - 1, False))
            start_all(grad_copies(j - 1))

        @pl.when((k == 1) & (j > early))
        def _():
            wait_all(grad_out(j - 1, True))

        turn(slot)

        @pl.when(j == 0)
        def _():
            add_bias_grad(slot)

        chunk(j, slot, mine, False, True)

        @pl.when(k == last)
        def _():
            stage[0] = acc1[:, cols_of(j)].astype(BF16)
            stage[1] = acc2[:, cols_of(j)].T.astype(BF16)

        @pl.when((k == last) & (j < early))
        def _():
            start_all(grad_out(j, False))

        @pl.when((k == last) & (j >= early))
        def _():
            start_all(grad_out(j, True))

        return carry

    lax.fori_loop(0, chunks * ep_size, far_step, 0)
    wait_all(grad_out(chunks - 1, True))
    for j in range(early):
        wait_all(grad_copies(j))
    for k in range(1, count):
        stat_copy(k).wait()
    total = slots[0]
    for k in range(1, count):
        total = total + slots[k]
    st_out[...] = total
    df_own().wait_send()
    for k in range(ep_size):
        xf_copy(k).wait_send()
    for k in range(1, ep_size):
        df_copy(k).wait_send()
        do_copy(k).wait_send()
        x_copy(k).wait_send()
        d_copy(k).wait_send()
        yo_copy(k).wait()
        dxo_copy(k).wait()
        y_copy(k).wait()


def exchange_call(mesh, xo, dos, xs, ds, w1, b1, w2, b2, stats, fchunk=FCHUNK):
    ep_size = mesh.shape["ep"]
    count = mesh.shape["dp"] * ep_size
    tiles, r, width = xs.shape
    hidden = w1.shape[-1]
    anyspec = pl.BlockSpec(memory_space=pl.ANY)
    vm = pl.BlockSpec(memory_space=pltpu.VMEM)
    rows = jax.ShapeDtypeStruct(xs.shape, BF16)
    both = jax.ShapeDtypeStruct((2 * tiles, r, width), BF16)
    g1h = jax.ShapeDtypeStruct((width, hidden // 2), BF16)
    g2h = jax.ShapeDtypeStruct((hidden // 2, width), BF16)
    out_shape = [both, rows, rows, g1h, g2h, g1h, g2h, g1h, g2h,
                 jax.ShapeDtypeStruct((1, hidden), F32), jax.ShapeDtypeStruct((1, width), F32), jax.ShapeDtypeStruct(stats.shape, F32)] + [rows] * 8
    out_specs = [anyspec] * 9 + [vm] * 3 + [anyspec] * 8
    dma = pltpu.SemaphoreType.DMA
    scratch = [
        pltpu.VMEM((width, hidden), BF16), pltpu.VMEM((hidden, width), BF16),
        pltpu.VMEM((width, hidden), F32), pltpu.VMEM((width, hidden), F32),
        pltpu.VMEM((2, r, width), BF16), pltpu.VMEM((2, r, width), BF16),
        pltpu.VMEM((width, r), BF16), pltpu.VMEM((width, r), BF16),
        pltpu.VMEM((r, width), F32), pltpu.VMEM((r, width), F32),
        pltpu.VMEM((r, width), BF16), pltpu.VMEM((r, width), BF16),
        pltpu.VMEM((2, fchunk, width), BF16), pltpu.VMEM((count,) + stats.shape, F32),
        dma((count,)), dma((count,)),
    ] + [dma((ep_size,))] * 16 + [dma((hidden // fchunk,))] * 4 + [dma((2,)), dma((2, 2)), dma((2,)), dma((2,))]
    flops = 14 * 2 * tiles * r * width * hidden
    return pl.pallas_call(
        functools.partial(exchange_body, ep_size, count, fchunk),
        in_specs=[anyspec] * 6 + [vm] * 3,
        out_specs=out_specs,
        out_shape=out_shape,
        scratch_shapes=scratch,
        compiler_params=pltpu.CompilerParams(vmem_limit_bytes=VMEM_CAP, collective_id=1, has_side_effects=True),
        cost_estimate=pl.CostEstimate(flops=flops, bytes_accessed=12 * tiles * r * width * 2, transcendentals=3 * tiles * r * hidden),
        name="exchange",
    )(xo, dos, xs, ds, w1, w2, b1[:, None, :], b2[:, None, :], stats)[:12]


def router_forward(x_loc, modality, router, expert_ids):
    num_experts = router.shape[1]
    logits = jnp.dot(x_loc, router, precision=lax.Precision.HIGHEST, preferred_element_type=F32)
    log_probs = jax.nn.log_softmax(logits, axis=-1)
    router_probs = jnp.exp(log_probs)
    expert_onehot = (expert_ids[:, None] == jnp.arange(num_experts)[None, :]).astype(F32)
    gate_prob = jnp.sum(router_probs * expert_onehot, axis=-1)
    mod_mask = jnp.stack([modality == 0, modality == 1]).astype(F32)
    entropy = -jnp.sum(router_probs * log_probs, axis=-1)
    local_stats = jnp.concatenate([jnp.dot(mod_mask, router_probs), jnp.dot(mod_mask, entropy)[:, None], jnp.sum(mod_mask, axis=1, keepdims=True)], axis=1)
    return log_probs, router_probs, expert_onehot, gate_prob, mod_mask, local_stats


def aux_from_stats(stats, num_experts):
    mod_count = stats[:, num_experts + 1]
    mean_probs = stats[:, :num_experts] / mod_count[:, None]
    aux_loss = jnp.sum(stats[:, num_experts] / mod_count) + jnp.sum(mean_probs * jnp.log(mean_probs))
    return aux_loss, mean_probs, mod_count


def router_backward(x_loc, router, log_probs, router_probs, expert_onehot, mod_mask, mean_probs, mod_count, d_gate):
    inv_count = jnp.dot(1.0 / mod_count, mod_mask)
    global_part = jnp.einsum("mt,me->te", mod_mask, jnp.log(mean_probs) / mod_count[:, None])
    d_probs = expert_onehot * d_gate[:, None] + global_part - log_probs * inv_count[:, None]
    d_logits = router_probs * (d_probs - jnp.sum(d_probs * router_probs, axis=-1, keepdims=True))
    d_router_part = jnp.einsum("tw,te->we", x_loc, d_logits, precision=lax.Precision.HIGHEST, preferred_element_type=F32)
    dx_router = jnp.einsum("te,we->tw", d_logits, router, precision=lax.Precision.HIGHEST, preferred_element_type=F32)
    return d_router_part, dx_router.astype(BF16)


def solution(mesh):
    token_spec = P(ALL_AXES)
    expert_spec = P("ep")
    swap = [(i, 1 - i) for i in range(2)]

    def local_step(x_loc, modality, router, expert_ids, priority, w_in, b_in, w_out, b_out, dy_loc):
        num_tokens, width = x_loc.shape
        num_experts = router.shape[1]
        capacity = num_tokens // num_experts
        half = num_experts // 2
        mine = lax.axis_index("dp")
        order = jnp.argsort(expert_ids * num_tokens + priority)
        counts = jnp.sum((expert_ids[:, None] == jnp.arange(num_experts)[None, :]).astype(jnp.int32), axis=0)
        starts = jnp.cumsum(counts) - counts
        x_slots, d_slots = slot_tables(order, starts, counts, capacity)

        def to_owner(table, slots):
            rows = jnp.take(table, slots, axis=0, mode="clip").reshape(half, capacity, width)
            return lax.all_to_all(rows, "ep", 0, 0, tiled=True)

        def pick(table, slots):
            return [r.reshape(half, capacity, width) for r in take_rows([table], slots, n_outs=2)]

        def swap_rows(rows):
            return lax.all_to_all(rows, "ep", 0, 0, tiled=True)

        xo_rows, x_rows = pick(x_loc, x_slots)
        x_other = swap_rows(xo_rows)
        x_rt, _ = lax.optimization_barrier((x_loc, xo_rows))
        log_probs, router_probs, expert_onehot, gate_prob, mod_mask, local_stats = router_forward(x_rt, modality, router, expert_ids)
        dy_f32 = dy_loc.astype(F32)
        d_tok = (gate_prob[:, None] * dy_f32).astype(BF16)
        do_rows, d_rows = pick(d_tok, d_slots)
        stats_block = jnp.pad(local_stats, ((0, 6), (0, 128 - num_experts - 2)))
        y_back, dx_other, dx_mine, g_in0, g_out0, g_in1, g_out1, far_in0, far_out0, gb_in, gb_out, stats_sum = exchange_call(mesh, x_other, do_rows, x_rows, d_rows, w_in, b_in, w_out, b_out, stats_block)
        aux_loss, mean_probs, mod_count = aux_from_stats(stats_sum[:2, :num_experts + 2], num_experts)
        dx_back = [r.reshape(half * capacity, width) for r in (dx_other, swap_rows(dx_mine))]
        y_back = y_back.reshape(num_experts * capacity, width)
        g_bias = jnp.concatenate([gb_in, gb_out], axis=1).astype(BF16)
        far_out1 = lax.ppermute(g_out1, "dp", swap)
        far_in1 = lax.ppermute(g_in1, "dp", swap)
        far_bias = lax.ppermute(g_bias, "dp", swap)

        def both(near, far):
            first = mine == 0
            return jnp.stack([jnp.where(first, near, far), jnp.where(first, far, near)])

        rank = jnp.argsort(order)
        ids = jnp.arange(num_experts)
        position = rank - jnp.sum(jnp.where(expert_ids[:, None] == ids[None, :], starts[None, :], 0), axis=1)
        place = jnp.where(lax.rem(expert_ids, 2) == mine, half, 0) + expert_ids // 2
        token_slot = jnp.where(position < capacity, place * capacity + position, num_experts * capacity)

        y_tok = take_rows([y_back], token_slot)[0].astype(F32)
        out_tokens = (gate_prob[:, None] * y_tok).astype(BF16)
        d_gate = jnp.sum(dy_f32 * y_tok, axis=-1)
        d_router_part, dx_router = router_backward(x_loc, router, log_probs, router_probs, expert_onehot, mod_mask, mean_probs, mod_count, d_gate)
        dx_router = lax.optimization_barrier(dx_router)
        dx_tokens = take_rows(dx_back, token_slot)[0] + dx_router
        dx_tokens, d_router_part = lax.optimization_barrier((dx_tokens, d_router_part))
        d_router = device_sum(d_router_part.T.reshape(-1, 128), mesh, 2).reshape(num_experts, width).T
        d_router, far_in1, far_out1, far_bias = lax.optimization_barrier((d_router, far_in1, far_out1, far_bias))
        d_w_in, d_w_out = join_grads((g_in0, g_in1), (far_in0, far_in1), (g_out0, g_out1), (far_out0, far_out1))
        bias = both(g_bias[0], far_bias[0])
        hidden = w_in.shape[-1]
        return (out_tokens, aux_loss, dx_tokens, d_router, d_w_in, bias[:, :hidden], d_w_out, bias[:, hidden:])

    return jax.shard_map(
        local_step,
        mesh=mesh,
        in_specs=(token_spec, token_spec, P(), token_spec, token_spec, expert_spec, expert_spec, expert_spec, expert_spec, token_spec),
        out_specs=(token_spec, P(), token_spec, P(), expert_spec, expert_spec, expert_spec, expert_spec),
        check_vma=False,
    )
```

time: 2210 us -> 719 us (0.33)
  blocking collectives: 1160 us -> 0 us
  Pallas kernels: 0 us -> 560 us
  matrix products: 419 us -> 44.4 us
  local copies, waits for them, and re-layouts: 378 us -> 10.1 us
  waiting for transfers between devices: 140 us -> 14.1 us
    psum x3 -> x0, blocking collectives: 1160 us -> none  [the longest x1 858 us: local_step(): expert_grads = lax.psum((d_w_in, d_b_in, d_w_out, d_b_out), 'dp')]
    pallas_call x0 -> x8, Pallas kernels: none -> 560 us  [the longest x1 415 us: exchange_call(): pl.pallas_call(functools.partial(exchange_body, ep_size, count, fchunk),...]
    dot_general x6 -> x0, matrix products: 372 us -> none  [the longest x1 106 us: local_step(): jnp.einsum('ecw,efw->ecf', d_recv, w_out, preferred_element_type=jnp.floa...]
    gather x7 -> x0, local copies, waits for them, and re-layouts: 220 us -> none  [the longest x2 45.5 us: route_tokens(): sort_order[jnp.minimum(starts[:, None] + slot_rank[None, :], num_tokens -...]
    all_to_all x4 -> x2, waiting for transfers between devices: 140 us -> 14.1 us  [swap_rows(): return lax.all_to_all(rows, 'ep', 0, 0, tiled=True)]
    convert_element_type x2 -> x0, local copies, waits for them, and re-layouts: 113 us -> none  [the longest x1 88.8 us: local_step(): expert_out.astype(jnp.bfloat16)]
    all_to_all x4 -> x0, local copies, waits for them, and re-layouts: 44.7 us -> none  [the longest x1 11.9 us: local_step(): d_back = lax.all_to_all(d_rows, 'ep', 1, 0, tiled=True)]
  transfers between devices with their start and end apart: 4 -> 5, of which waited for: 1 -> 1; matrix products, arithmetic and copies ran while one was open for 2% -> 14% of each run, Pallas kernels for 0% -> 15%
where the time goes in v2:
time: 719 us; the launch traced here: 713 us
  Pallas kernels  560 us (78%)
  other arithmetic  65.4 us (9%)
  matrix products  44.4 us (6%)
  starting transfers between devices  15.5 us (2%)
  waiting for transfers between devices  14.1 us (2%)
  local copies, waits for them, and re-layouts  10.1 us (1%)
    pallas_call x1, Pallas kernels, exchange_call(): pl.pallas_call(functools.partial(exchange_body, ep_size, count, fchunk),...  415 us
    pallas_call x4, Pallas kernels, take_rows(): pl.pallas_call(functools.partial(take_body, len(tables), n_outs, rows_in,...  118 us
    dot_general x1, matrix products, router_backward(): jnp.einsum('te,we->tw', d_logits, router, precision=lax.Precision.HIGHEST...  22.3 us
    reduce_sum x1, other arithmetic, local_step(): d_gate = jnp.sum(dy_f32 * y_tok, axis=-1)  17.3 us
    pallas_call x1, Pallas kernels, device_sum(): pl.pallas_call(functools.partial(sum_kernel, mesh.shape['ep'], count), in...  16.2 us
  transfers between devices with their start and end apart: 5, of which 1 were waited for; matrix products, arithmetic and copies ran while one was open for 14% of the time, Pallas kernels for 15%

profile of v2, /device:TPU:0, one launch (start us, length us, event | category | flops | bytes accessed | tf_op | source)
XLA Modules:
  0.0 713.1 jit_solution(6193870398415967300)
XLA Ops:
  0.6 0.9 convert_reduce_fusion
  2.4 0.8 multiply_add_fusion
  3.2 6.8 sort.31
  11.2 1.6 slots.1
  12.8 1.4 fusion.10
  14.3 29.9 %take_rows.4 = (bf16[4096,768]{1,0:T(8,128)(2,1)}, bf16[4096,768]{1,0:T(8,128)(2,1)}) custom-call(s32[8192]{0:T(1024)} %get-tuple-element.82.q_ref, bf16[8192,768]{1,0:T(8,128)(2,1)} %refs_0_.1), custom_call_target="tpu_custom_call" | custom-call | flops 268435456 | bytes 25165824 | tf_op jit(solution)/shard_map/take_rows/pallas_call | solution.py:183
  44.2 5.8 all-to-all-start
  51.7 12.8 %fusion.40 = (f32[8192]{0:T(1024)S(1)}, f32[8192,16]{0,1:T(8,128)S(1)}) fusion(bf16[8192,768]{1,0:T(8,128)(2,1)} %refs_0_.1, f32[768,16]{0,1:T(8,128)S(1)} %copy-done), kind=kOutput, calls=%fused_computation.105 | convolution fusion | flops 1208082432 | bytes 13189120 | tf_op jit(solution)/shard_map/dot_general | solution.py:576
  65.0 11.7 %fusion.refs_0_ = bf16[8192,768]{1,0:T(8,128)(2,1)} fusion(bf16[8192,768]{1,0:T(8,128)(2,1)} %param.19, f32[8192]{0:T(1024)S(1)} %get-tuple-element.67), kind=kLoop, calls=%fused_computation.3 | loop fusion | flops 18874368 | bytes 25198592 | tf_op jit(solution)/shard_map/convert_element_type | solution.py:635
  76.7 29.8 %take_rows.5 = (bf16[4096,768]{1,0:T(8,128)(2,1)}, bf16[4096,768]{1,0:T(8,128)(2,1)}) custom-call(s32[8192]{0:T(1024)} %get-tuple-element.83.q_ref, bf16[8192,768]{1,0:T(8,128)(2,1)} %fusion.refs_0_), custom_call_target="tpu_custom_call" | custom-call | flops 268435456 | bytes 25165824 | tf_op jit(solution)/shard_map/take_rows/pallas_call | solution.py:183
  107.0 0.7 select_maximum_fusion.st_ref
  107.7 14.1 %all-to-all-done.xo = bf16[8,512,768]{2,1,0:T(8,128)(2,1)} async-done(((bf16[8,512,768]{2,1,0:T(8,128)(2,1)}), bf16[8,512,768]{2,1,0:T(8,128)(2,1)}, u32[]{:S(2)}, u32[]{:S(2)}) %all-to-all-start) | async-done | bytes 6291488 | tf_op jit(solution)/shard_map/all_to_all | solution.py:628
  121.7 414.9 %exchange.1 = (bf16[16,512,768]{2,1,0:T(8,128)(2,1)}, bf16[8,512,768]{2,1,0:T(8,128)(2,1)}, bf16[8,512,768]{2,1,0:T(8,128)(2,1)}, bf16[768,1536]{1,0:T(8,128)(2,...) custom-call(bf16[8,512,768]{2,1,0:T(8,128)(2,1)} %all-to-all-done.xo, ...), custom_call_target="tpu_custom_call" | custom-call | flops 270582939648 | bytes 75497472 | tf_op jit(solution)/shard_map/exchange/pallas_call | solution.py:562
  536.6 6.1 all-to-all-start.1
  542.8 6.8 sort.32
  549.7 0.7 fusion.16.q_ref
  550.5 1.5 collective-permute-start.2
  552.6 1.5 collective-permute-start.1
  554.0 29.0 %take_rows.6 = bf16[8192,768]{1,0:T(8,128)(2,1)} custom-call(s32[8192]{0:T(1024)} %fusion.16.q_ref, bf16[8192,768]{1,0:T(8,128)(2,1)} %bitcast.75), custom_call_target="tpu_custom_call" | custom-call | flops 268435456 | bytes 25165824 | tf_op jit(solution)/shard_map/take_rows/pallas_call | solution.py:183
  583.5 17.3 %fusion.2 = (f32[8192]{0:T(1024)S(1)}, bf16[8192,768]{1,0:T(8,128)(2,1)}) fusion(bf16[8192,768]{1,0:T(8,128)(2,1)} %take_rows.6, bf16[8192,768]{1,0:T(8,128)(2,1)} %param.19, f32[8192]{0:T(1024)S(1)} %copy-done.14), kind=kLoop, calls=%fused_computation.5 | loop fusion | flops 37740544 | bytes 37814272 | tf_op jit(solution)/shard_map/reduce_sum | solution.py:659
  601.2 22.3 %convolution_convert_fusion = bf16[8192,768]{1,0:T(8,128)(2,1)} fusion(f32[768,16]{0,1:T(8,128)S(1)} %copy-done, f32[8192,16]{0,1:T(8,128)S(1)} %get-tuple-element.81, f32[8192]{0:T(1024)S(1)} %get-tuple-element.80, f32[8192,16]{0,1:T(8,128)S(1)} %copy-done.6, f32[8192]{0:T(1024)S(1)} %copy-done.10, f32[8192]{0:T(1024)S(1)} %copy-done.8), kind=kOutput, calls=%fused_computation.6 | convolution fusion | flops 1214775296 | bytes 13778944 | tf_op jit(solution)/shard_map/te,we->tw/dot_general | solution.py:600
  624.1 0.7 fusion.35
  626.1 8.2 %convolution_bitcast_fusion = f32[768,16]{0,1:T(8,128)S(1)} fusion(bf16[8192,768]{1,0:T(8,128)(2,1)} %refs_0_.1, f32[8192,16]{0,1:T(8,128)S(1)} %get-tuple-element.81, f32[8192]{0:T(1024)S(1)} %get-tuple-element.80, f32[8192,16]{0,1:T(8,128)S(1)} %copy-done.6, f32[8192]{0:T(1024)S(1)} %copy-done.10, f32[8192]{0:T(1024)S(1)} %copy-done.8), kind=kOutput, calls=%fused_computation.9 | convolution fusion | flops 1208483840 | bytes 13778944 | tf_op jit(solution)/shard_map/tw,te->we/dot_general | solution.py:599
  634.3 28.9 %take_rows.7 = bf16[8192,768]{1,0:T(8,128)(2,1)} custom-call(s32[8192]{0:T(1024)} %fusion.16.q_ref, bf16[4096,768]{1,0:T(8,128)(2,1)} %bitcast.77, bf16[4096,768]{1,0:T(8,128)(2,1)} %bitcast.16.refs_1_), custom_call_target="tpu_custom_call" | custom-call | flops 268435456 | bytes 25165824 | tf_op jit(solution)/shard_map/take_rows/pallas_call | solution.py:183
  663.2 14.2 %add.63 = bf16[8192,768]{1,0:T(8,128)(2,1)} add(bf16[8192,768]{1,0:T(8,128)(2,1)} %take_rows.7, bf16[8192,768]{1,0:T(8,128)(2,1)} %convolution_convert_fusion) | non-fusion elementwise | flops 6291456 | bytes 37748736 | tf_op jit(solution)/shard_map/add | solution.py:662
  678.1 16.2 %device_sum.1 = f32[96,128]{1,0:T(8,128)} custom-call(f32[96,128]{1,0:T(8,128)} %reshape.135.x_ref), custom_call_target="tpu_custom_call" | custom-call | flops 10000000 | bytes 1000000 | tf_op jit(solution)/shard_map/device_sum/pallas_call | solution.py:94
  694.3 1.4 reshape.136
  696.4 0.6 fusion.34
  697.0 1.7 copy-done.2
  698.7 1.7 copy-done.3
  700.3 1.7 copy-done.4
  702.0 9.7 %join_grads.1 = (bf16[2,768,3072]{2,1,0:T(8,128)(2,1)}, bf16[2,3072,768]{2,1,0:T(8,128)(2,1)}) custom-call(bf16[768,1536]{1,0:T(8,128)(2,1)S(1)} %copy-done.1, bf16[768,1536]{1,0:T(8,128)(2,1)S(1)} %copy-done.3, bf16[768,1536]{1,0:T(8,128)(2,1)} %get-tuple-element.52.refs_2_, bf16[768,1536]{1,0:T(8,128)(2,1)} %collective-permute-done.refs_3_, ...), custom_call_target="tpu_custom_call" | custom-call | flops 10000000 | bytes 37748736 | tf_op jit(solution)/shard_map/join_grads/pallas_call | solution.py:221
  (88 shorter events, 8.2 us)
Async XLA Ops:
  0.6 51.1 %copy-start = (f32[768,16]{0,1:T(8,128)S(1)}, f32[768,16]{0,1:T(8,128)}, u32[]{:S(2)}) copy-start(f32[768,16]{0,1:T(8,128)} %param.12) | copy-start | bytes 147460
  1.8 1.4 copy-start.25
  10.0 0.6 copy-start.15
  14.3 35.8 %copy-start.23 = (bf16[2,768]{1,0:T(2,128)(2,1)S(1)}, bf16[2,768]{1,0:T(2,128)(2,1)}, u32[]{:S(2)}) copy-start(bf16[2,768]{1,0:T(2,128)(2,1)} %param.18) | copy-start | bytes 9220
  14.3 36.4 %copy-start.19 = (s32[8192]{0:T(1024)S(1)}, s32[8192]{0:T(1024)}, u32[]{:S(2)}) copy-start(s32[8192]{0:T(1024)} %param.11) | copy-start | bytes 98308
  14.3 36.4 %copy-start.21 = (bf16[2,3072]{1,0:T(2,128)(2,1)S(1)}, bf16[2,3072]{1,0:T(2,128)(2,1)}, u32[]{:S(2)}) copy-start(bf16[2,3072]{1,0:T(2,128)(2,1)} %param.16) | copy-start | bytes 36868
  44.2 20.5 %copy-start.11 = (s32[8192]{0:T(1024)S(1)}, s32[8192]{0:T(1024)}, u32[]{:S(2)}) copy-start(s32[8192]{0:T(1024)} %param.13) | copy-start | bytes 98308
  44.2 77.5 %all-to-all-start = ((bf16[8,512,768]{2,1,0:T(8,128)(2,1)}), bf16[8,512,768]{2,1,0:T(8,128)(2,1)}, u32[]{:S(2)}, u32[]{:S(2)}) async-start(bf16[8,512,768]{2,1,0:T(8,128)(2,1)} %bitcast.76), calls=%async_computation | async-start | bytes 12582912 | tf_op jit(solution)/shard_map/all_to_all | solution.py:628
  51.6 55.1 %copy-start.17 = (pred[2,8192]{1,0:T(4,128)(4,1)}, pred[2,8192]{1,0:T(4,128)(4,1)S(1)}, u32[]{:S(2)}) copy-start(pred[2,8192]{1,0:T(4,128)(4,1)S(1)} %get-tuple-element.71) | copy-start | bytes 49156
  64.5 42.2 %copy-start.5 = (f32[8192,16]{0,1:T(8,128)}, f32[8192,16]{0,1:T(8,128)S(1)}, u32[]{:S(2)}) copy-start(f32[8192,16]{0,1:T(8,128)S(1)} %get-tuple-element.79) | copy-start | bytes 1572868
  64.5 42.2 %copy-start.7 = (f32[8192]{0:T(1024)}, f32[8192]{0:T(1024)S(1)}, u32[]{:S(2)}) copy-start(f32[8192]{0:T(1024)S(1)} %get-tuple-element.78) | copy-start | bytes 98308
  64.7 42.1 %copy-start.9 = (f32[8192]{0:T(1024)}, f32[8192]{0:T(1024)S(1)}, u32[]{:S(2)}) copy-start(f32[8192]{0:T(1024)S(1)} %log.13) | copy-start | bytes 98308
  65.0 11.7 %copy-start.13 = (f32[8192]{0:T(1024)}, f32[8192]{0:T(1024)S(1)}, u32[]{:S(2)}) copy-start(f32[8192]{0:T(1024)S(1)} %get-tuple-element.67) | copy-start | bytes 98308
  536.6 6.2 copy-start.16
  536.6 13.0 %copy-start.12 = (s32[8192]{0:T(1024)S(1)}, s32[8192]{0:T(1024)}, u32[]{:S(2)}) copy-start(s32[8192]{0:T(1024)} %param.13) | copy-start | bytes 98308
  536.6 13.0 %copy-start.26 = (s32[16]{0:T(128)S(1)}, s32[16]{0:T(128)}, u32[]{:S(2)}) copy-start(s32[16]{0:T(128)} %copy-done.25) | copy-start | bytes 196
  536.6 13.8 %copy-start.22 = (f32[1,768]{1,0:T(1,128)S(1)}, f32[1,768]{1,0:T(1,128)}, u32[]{:S(2)}) copy-start(f32[1,768]{1,0:T(1,128)} %get-tuple-element.55) | copy-start | bytes 9220
  536.6 13.8 %copy-start.20 = (f32[1,3072]{1,0:T(1,128)S(1)}, f32[1,3072]{1,0:T(1,128)}, u32[]{:S(2)}) copy-start(f32[1,3072]{1,0:T(1,128)} %get-tuple-element.54) | copy-start | bytes 36868
  536.6 97.7 %all-to-all-start.1 = ((bf16[8,512,768]{2,1,0:T(8,128)(2,1)}), bf16[8,512,768]{2,1,0:T(8,128)(2,1)}, u32[]{:S(2)}, u32[]{:S(2)}) async-start(bf16[8,512,768]{2,1,0:T(8,128)(2,1)} %get-tuple-element.49), calls=%async_computation.1 | async-start | bytes 12582912 | tf_op jit(solution)/shard_map/all_to_all | solution.py:628
  550.5 145.2 %collective-permute-start.2 = (bf16[1,3840]{1,0:T(2,128)(2,1)S(1)}, bf16[1,3840]{1,0:T(2,128)(2,1)S(1)}, u32[]{:S(2)}, u32[]{:S(2)}) collective-permute-start(bf16[1,3840]{1,0:T(2,128)(2,1)S(1)} %pad_maximum_fusion), channel_id=1, source_target_pairs={{0,8},{8,0},{1,9},{9,1},{2,10},{10,2},{3,11},{11,3},{4,12},{12,4},... | collective-permute-start | bytes 23048 | tf_op jit(solution)/shard_map/ppermute | solution.py:645
  552.0 143.7 %collective-permute-start = (bf16[768,1536]{1,0:T(8,128)(2,1)}, bf16[768,1536]{1,0:T(8,128)(2,1)}, u32[]{:S(2)}, u32[]{:S(2)}) collective-permute-start(bf16[768,1536]{1,0:T(8,128)(2,1)} %get-tuple-element.52.refs_2_), channel_id=1, source_target_pairs={{0,8},{8,0},{1,9},{9,1},{2,10},{10,2},{3,11},{11,3},{4,12},{12,4},... | collective-permute-start | bytes 7077896 | tf_op jit(solution)/shard_map/ppermute | solution.py:644
  552.6 143.2 %collective-permute-start.1 = (bf16[1536,768]{1,0:T(8,128)(2,1)}, bf16[1536,768]{1,0:T(8,128)(2,1)}, u32[]{:S(2)}, u32[]{:S(2)}) collective-permute-start(bf16[1536,768]{1,0:T(8,128)(2,1)} %get-tuple-element.53.refs_6_), channel_id=1, source_target_pairs={{0,8},{8,0},{1,9},{9,1},{2,10},{10,2},{3,11},{11,3},{4,12},{12,4},... | collective-permute-start | bytes 7077896 | tf_op jit(solution)/shard_map/ppermute | solution.py:643
  554.0 29.0 %copy-start.24 = (f32[8,128]{1,0:T(8,128)S(1)}, f32[8,128]{1,0:T(8,128)}, u32[]{:S(2)}) copy-start(f32[8,128]{1,0:T(8,128)} %get-tuple-element.47) | copy-start | bytes 12292
  554.0 29.2 %copy-start.18 = (pred[2,8192]{1,0:T(4,128)(4,1)S(1)}, pred[2,8192]{1,0:T(4,128)(4,1)}, u32[]{:S(2)}) copy-start(pred[2,8192]{1,0:T(4,128)(4,1)} %copy-done.17) | copy-start | bytes 49156
  554.0 29.4 %copy-start.14 = (f32[8192]{0:T(1024)S(1)}, f32[8192]{0:T(1024)}, u32[]{:S(2)}) copy-start(f32[8192]{0:T(1024)} %copy-done.13) | copy-start | bytes 98308
  583.4 17.3 %copy-start.6 = (f32[8192,16]{0,1:T(8,128)S(1)}, f32[8192,16]{0,1:T(8,128)}, u32[]{:S(2)}) copy-start(f32[8192,16]{0,1:T(8,128)} %copy-done.5) | copy-start | bytes 1572868
  583.4 17.3 %copy-start.8 = (f32[8192]{0:T(1024)S(1)}, f32[8192]{0:T(1024)}, u32[]{:S(2)}) copy-start(f32[8192]{0:T(1024)} %copy-done.7) | copy-start | bytes 98308
  583.4 17.3 %copy-start.10 = (f32[8192]{0:T(1024)S(1)}, f32[8192]{0:T(1024)}, u32[]{:S(2)}) copy-start(f32[8192]{0:T(1024)} %copy-done.9) | copy-start | bytes 98308
  663.2 33.8 %copy-start.1 = (bf16[768,1536]{1,0:T(8,128)(2,1)S(1)}, bf16[768,1536]{1,0:T(8,128)(2,1)}, u32[]{:S(2)}) copy-start(bf16[768,1536]{1,0:T(8,128)(2,1)} %get-tuple-element.57.refs_0_) | copy-start | bytes 7077892
  697.0 1.7 copy-start.2
  698.7 1.7 copy-start.3
  700.3 1.7 copy-start.4

commit v3 on v2

--- a/solution.py
+++ b/solution.py
@@ -5,6 +5,7 @@
 from jax.experimental import pallas as pl
 from jax.experimental.pallas import tpu as pltpu
 from jax.sharding import PartitionSpec as P
+
 
 F32 = jnp.float32
 BF16 = jnp.bfloat16
@@ -61,51 +62,60 @@
     return xs.reshape(-1), ds.reshape(-1)
 
 
-def sum_kernel(ep_size, count, x_ref, out_ref, slots, send_sem, recv_sem):
+def sum_kernel(ep_size, count, x_ref, out_ref, slots, part, send_a, recv_a, send_b, recv_b):
     dp_me, ep_me = lax.axis_index("dp"), lax.axis_index("ep")
     me = dp_me * ep_size + ep_me
 
     def peer(k):
-        p = lax.rem(me + k, count)
-        return (p // ep_size, lax.rem(p, ep_size))
+        return lax.rem(me + k, count)
+
+    def to(src, dst, send, recv, p):
+        return pltpu.make_async_remote_copy(src_ref=src, dst_ref=dst, send_sem=send, recv_sem=recv,
+                                            device_id=(p // ep_size, lax.rem(p, ep_size)), device_id_type=MESH_ID)
 
     barrier = pltpu.get_barrier_semaphore()
     for k in range(1, count):
-        pl.semaphore_signal(barrier, inc=1, device_id=peer(k), device_id_type=MESH_ID)
+        p = peer(k)
+        pl.semaphore_signal(barrier, inc=1, device_id=(p // ep_size, lax.rem(p, ep_size)), device_id_type=MESH_ID)
     pl.semaphore_wait(barrier, count - 1)
-    copies = []
-    for k in range(1, count):
-        c = pltpu.make_async_remote_copy(
-            src_ref=x_ref, dst_ref=slots.at[me], send_sem=send_sem.at[k], recv_sem=recv_sem.at[k],
-            device_id=peer(k), device_id_type=MESH_ID)
+    scatter = [to(x_ref.at[peer(k)], slots.at[me], send_a.at[k], recv_a.at[k], peer(k)) for k in range(1, count)]
+    for c in scatter:
         c.start()
-        copies.append(c)
-    slots[me] = x_ref[...]
-    for c in copies:
+    slots[me] = x_ref[me]
+    for c in scatter:
         c.wait()
     total = slots[0]
     for k in range(1, count):
         total = total + slots[k]
-    out_ref[...] = total
+    part[...] = total
+    spread = [to(part, out_ref.at[me], send_b.at[k], recv_b.at[k], peer(k)) for k in range(1, count)]
+    for c in spread:
+        c.start()
+    out_ref[me] = total
+    for c in spread:
+        c.wait()
 
 
 def device_sum(x, mesh, collective_id):
     count = mesh.shape["dp"] * mesh.shape["ep"]
+    dma = pltpu.SemaphoreType.DMA((count,))
     return pl.pallas_call(
         functools.partial(sum_kernel, mesh.shape["ep"], count),
         in_specs=[pl.BlockSpec(memory_space=pltpu.VMEM)],
         out_specs=pl.BlockSpec(memory_space=pltpu.VMEM),
         out_shape=jax.ShapeDtypeStruct(x.shape, F32),
-        scratch_shapes=[pltpu.VMEM((count,) + x.shape, F32), pltpu.SemaphoreType.DMA((count,)), pltpu.SemaphoreType.DMA((count,))],
+        scratch_shapes=[pltpu.VMEM(x.shape, F32), pltpu.VMEM(x.shape[1:], F32), dma, dma, dma, dma],
         compiler_params=pltpu.CompilerParams(collective_id=collective_id, has_side_effects=True),
         cost_estimate=pl.CostEstimate(flops=10_000_000, bytes_accessed=1_000_000, transcendentals=0),
         name="device_sum",
     )(x)
 
 
-def take_body(n_tables, n_outs, rows_in, rows_out, chunk, q_ref, *refs):
-    tables, results = refs[:n_tables], refs[n_tables:n_tables + n_outs]
-    wide, inbuf, outs, outbuf, in_sem, out_sem = refs[n_tables + n_outs:]
+def take_body(n_tables, n_outs, added, rows_in, rows_out, chunk, q_ref, *refs):
+    tables, extra, results = refs[:n_tables], refs[n_tables:n_tables + added], refs[n_tables + added:n_tables + added + n_outs]
+    wide, inbuf, outs, outbuf, in_sem, out_sem = refs[n_tables + added + n_outs:][:6]
+    if added:
+        addbuf, add_sem = refs[-2:]
     width = inbuf.shape[-1]
     parts = width // 128
     per_table = rows_in // chunk // n_tables
@@ -121,15 +131,15 @@
         load(c).wait()
 
         def widen(g, carry, c=c):
-            for u in range(2):
-                v = inbuf[c % 2, pl.ds(pl.multiple_of(g * 32 + u * 16, 16), 16), :].astype(F32)
-                base = (c * chunk // 8 + g * 4 + u * 2) * 8 * parts
+            for u in range(4):
+                v = inbuf[c % 2, pl.ds(pl.multiple_of(g * 64 + u * 16, 16), 16), :].astype(F32)
+                base = (c * chunk // 8 + g * 8 + u * 2) * 8 * parts
                 for hh in range(2):
                     for k in range(parts):
                         wide[pl.ds(pl.multiple_of(base + (hh * parts + k) * 8, 8), 8), :] = v[hh * 8:hh * 8 + 8, k * 128:(k + 1) * 128]
             return carry
 
-        lax.fori_loop(0, chunk // 32, widen, 0)
+        lax.fori_loop(0, chunk // 64, widen, 0)
     wide[rows_in * parts:, :] = jnp.zeros((8 * parts, 128), F32)
 
     steps = rows_out // chunk // n_outs
@@ -138,30 +148,49 @@
         def store(c, slot):
             return pltpu.make_async_copy(outbuf.at[slot], out.at[pl.ds(c * chunk, chunk), :], out_sem.at[slot])
 
+        def addend(c, slot):
+            return pltpu.make_async_copy(extra[0].at[pl.ds(c * chunk, chunk), :], addbuf.at[slot], add_sem.at[slot])
+
+        if added:
+            addend(0, 0).start()
+
         def chunk_step(c, carry):
             slot = lax.rem(c, 2)
-
-            def rows(g, carry):
+            if added:
+                @pl.when(c + 1 < steps)
+                def _():
+                    addend(c + 1, lax.rem(c + 1, 2)).start()
+
+                addend(c, slot).wait()
+
+            @pl.when(c >= 2)
+            def _():
+                store(c - 2, slot).wait()
+
+            def rows(g):
                 at = [q_ref[(o * steps + c) * chunk + g * 32 + j] for j in range(32)]
                 got = [wide[pl.ds(q, parts, stride=8), :] for q in at]
                 for j in range(32):
                     outs[pl.ds((g * 4 + j // 8) * 8 * parts + j % 8, parts, stride=8), :] = got[j]
-                return carry
-
-            lax.fori_loop(0, chunk // 32, rows, 0)
-
-            @pl.when(c >= 2)
-            def _():
-                store(c - 2, slot).wait()
-
-            def narrow(g, carry):
+
+            def narrow(g):
                 for u in range(2):
                     base = (g * 4 + u * 2) * 8 * parts
                     v = [jnp.concatenate([outs[pl.ds(pl.multiple_of(base + (hh * parts + k) * 8, 8), 8), :] for hh in range(2)], axis=0) for k in range(parts)]
-                    outbuf[slot, pl.ds(pl.multiple_of(g * 32 + u * 16, 16), 16), :] = jnp.concatenate(v, axis=1).astype(BF16)
+                    at = pl.ds(pl.multiple_of(g * 32 + u * 16, 16), 16)
+                    row = jnp.concatenate(v, axis=1)
+                    if added:
+                        row = row + addbuf[slot, at, :].astype(F32)
+                    outbuf[slot, at, :] = row.astype(BF16)
+
+            def both_steps(g, carry):
+                narrow(g - 1)
+                rows(g)
                 return carry
 
-            lax.fori_loop(0, chunk // 32, narrow, 0)
+            rows(0)
+            lax.fori_loop(1, chunk // 32, both_steps, 0)
+            narrow(chunk // 32 - 1)
             store(c, slot).start()
             return carry
 
@@ -173,7 +202,8 @@
         fill(o, out)
 
 
-def take_rows(tables, index, n_outs=1, chunk=512):
+def take_rows(tables, index, n_outs=1, chunk=1024, addend=None):
+    more = [] if addend is None else [addend]
     rows_in = sum(t.shape[0] for t in tables)
     width = tables[0].shape[1]
     parts = width // 128
@@ -181,17 +211,18 @@
     q = (index // 8) * (8 * parts) + index % 8
     anyspec = pl.BlockSpec(memory_space=pl.ANY)
     return pl.pallas_call(
-        functools.partial(take_body, len(tables), n_outs, rows_in, rows_out, chunk),
+        functools.partial(take_body, len(tables), n_outs, len(more), rows_in, rows_out, chunk),
         grid_spec=pltpu.PrefetchScalarGridSpec(
-            num_scalar_prefetch=1, grid=(1,), in_specs=[anyspec] * len(tables), out_specs=[anyspec] * n_outs,
+            num_scalar_prefetch=1, grid=(1,), in_specs=[anyspec] * (len(tables) + len(more)), out_specs=[anyspec] * n_outs,
             scratch_shapes=[pltpu.VMEM(((rows_in + 8) * parts, 128), F32), pltpu.VMEM((2, chunk, width), BF16),
                             pltpu.VMEM((chunk * parts, 128), F32), pltpu.VMEM((2, chunk, width), BF16),
-                            pltpu.SemaphoreType.DMA((2,)), pltpu.SemaphoreType.DMA((2,))]),
+                            pltpu.SemaphoreType.DMA((2,)), pltpu.SemaphoreType.DMA((2,))]
+            + [pltpu.VMEM((2, chunk, width), BF16), pltpu.SemaphoreType.DMA((2,))] * len(more)),
         out_shape=[jax.ShapeDtypeStruct((rows_out // n_outs, width), BF16)] * n_outs,
         compiler_params=pltpu.CompilerParams(vmem_limit_bytes=VMEM_CAP),
         cost_estimate=pl.CostEstimate(flops=rows_out * 4096 * 8, bytes_accessed=2 * (rows_in + rows_out) * width, transcendentals=0),
         name="take_rows",
-    )(q, *tables)
+    )(q, *tables, *more)
 
 
 def join_body(*refs):
@@ -237,7 +268,6 @@
                   w1, w2, acc1, acc2, xv, dv, xt, dt, yacc, dxacc, ystage, dxstage, stage, slots,
                   st_send, st_recv, do_send, do_recv, x_send, x_recv, d_send, d_recv, xf_send, xf_recv, df_send, df_recv,
                   yo_send, yo_recv, dxo_send, dxo_recv, y_send, y_recv, g1_send, g1_recv, g2_send, g2_recv, w_sem, in_sem, out_sem, g_sem):
-    width = w1.shape[0]
     hidden = w1.shape[1]
     mine, e = lax.axis_index("dp"), lax.axis_index("ep")
     me = mine * ep_size + e
@@ -446,7 +476,6 @@
 
     chunks = hidden // fchunk
     early = chunks // 2
-    half = early * fchunk
 
     def cols_of(j):
         return pl.ds(pl.multiple_of(j * fchunk, fchunk), fchunk)
@@ -571,9 +600,18 @@
     )(xo, dos, xs, ds, w1, w2, b1[:, None, :], b2[:, None, :], stats)[:12]
 
 
+def three_parts(v):
+    high = lax.reduce_precision(v, 8, 7)
+    rest = v - high
+    mid = lax.reduce_precision(rest, 8, 7)
+    return high.astype(BF16), mid.astype(BF16), (rest - mid).astype(BF16)
+
+
 def router_forward(x_loc, modality, router, expert_ids):
     num_experts = router.shape[1]
-    logits = jnp.dot(x_loc, router, precision=lax.Precision.HIGHEST, preferred_element_type=F32)
+    high, mid, low = three_parts(router)
+    pieces = jnp.dot(x_loc, jnp.concatenate([high, mid, low], axis=1), preferred_element_type=F32)
+    logits = (pieces[:, 2 * num_experts:] + pieces[:, num_experts:2 * num_experts]) + pieces[:, :num_experts]
     log_probs = jax.nn.log_softmax(logits, axis=-1)
     router_probs = jnp.exp(log_probs)
     expert_onehot = (expert_ids[:, None] == jnp.arange(num_experts)[None, :]).astype(F32)
@@ -596,8 +634,14 @@
     global_part = jnp.einsum("mt,me->te", mod_mask, jnp.log(mean_probs) / mod_count[:, None])
     d_probs = expert_onehot * d_gate[:, None] + global_part - log_probs * inv_count[:, None]
     d_logits = router_probs * (d_probs - jnp.sum(d_probs * router_probs, axis=-1, keepdims=True))
-    d_router_part = jnp.einsum("tw,te->we", x_loc, d_logits, precision=lax.Precision.HIGHEST, preferred_element_type=F32)
-    dx_router = jnp.einsum("te,we->tw", d_logits, router, precision=lax.Precision.HIGHEST, preferred_element_type=F32)
+    num_experts = router.shape[1]
+    d1, d2, d3 = three_parts(d_logits)
+    r1, r2, r3 = three_parts(router)
+    pieces = jnp.einsum("tw,te->we", x_loc, jnp.concatenate([d1, d2, d3], axis=1), preferred_element_type=F32)
+    d_router_part = (pieces[:, 2 * num_experts:] + pieces[:, num_experts:2 * num_experts]) + pieces[:, :num_experts]
+    d_wide = jnp.concatenate([d1, d1, d2, d2, d1, d3], axis=1)
+    r_wide = jnp.concatenate([r1, r2, r1, r2, r3, r1], axis=1)
+    dx_router = jnp.einsum("te,we->tw", d_wide, r_wide, preferred_element_type=F32)
     return d_router_part, dx_router.astype(BF16)
 
 
@@ -617,27 +661,33 @@
         starts = jnp.cumsum(counts) - counts
         x_slots, d_slots = slot_tables(order, starts, counts, capacity)
 
-        def to_owner(table, slots):
-            rows = jnp.take(table, slots, axis=0, mode="clip").reshape(half, capacity, width)
-            return lax.all_to_all(rows, "ep", 0, 0, tiled=True)
-
-        def pick(table, slots):
-            return [r.reshape(half, capacity, width) for r in take_rows([table], slots, n_outs=2)]
+        def pick(table, slots, n_outs):
+            return [r.reshape(half, capacity, width) for r in take_rows([table], slots, n_outs=n_outs)]
 
         def swap_rows(rows):
             return lax.all_to_all(rows, "ep", 0, 0, tiled=True)
 
-        xo_rows, x_rows = pick(x_loc, x_slots)
+        first = half * capacity
+        xo_rows = pick(x_loc, x_slots[:first], 1)[0]
         x_other = swap_rows(xo_rows)
         x_rt, _ = lax.optimization_barrier((x_loc, xo_rows))
         log_probs, router_probs, expert_onehot, gate_prob, mod_mask, local_stats = router_forward(x_rt, modality, router, expert_ids)
         dy_f32 = dy_loc.astype(F32)
         d_tok = (gate_prob[:, None] * dy_f32).astype(BF16)
-        do_rows, d_rows = pick(d_tok, d_slots)
+        do_rows, d_rows = pick(d_tok, d_slots, 2)
+        x_later, _ = lax.optimization_barrier((x_slots[first:], gate_prob))
+        x_rows = pick(x_loc, x_later, 1)[0]
         stats_block = jnp.pad(local_stats, ((0, 6), (0, 128 - num_experts - 2)))
+        rank = jnp.argsort(order)
+        ids = jnp.arange(num_experts)
+        position = rank - jnp.sum(jnp.where(expert_ids[:, None] == ids[None, :], starts[None, :], 0), axis=1)
+        place = jnp.where(lax.rem(expert_ids, 2) == mine, half, 0) + expert_ids // 2
+        token_slot = jnp.where(position < capacity, place * capacity + position, num_experts * capacity)
+        stats_block, token_slot = lax.optimization_barrier((stats_block, token_slot))
         y_back, dx_other, dx_mine, g_in0, g_out0, g_in1, g_out1, far_in0, far_out0, gb_in, gb_out, stats_sum = exchange_call(mesh, x_other, do_rows, x_rows, d_rows, w_in, b_in, w_out, b_out, stats_block)
         aux_loss, mean_probs, mod_count = aux_from_stats(stats_sum[:2, :num_experts + 2], num_experts)
-        dx_back = [r.reshape(half * capacity, width) for r in (dx_other, swap_rows(dx_mine))]
+        dx_returned = swap_rows(dx_mine)
+        dx_back = [r.reshape(half * capacity, width) for r in (dx_other, dx_returned)]
         y_back = y_back.reshape(num_experts * capacity, width)
         g_bias = jnp.concatenate([gb_in, gb_out], axis=1).astype(BF16)
         far_out1 = lax.ppermute(g_out1, "dp", swap)
@@ -648,20 +698,16 @@
             first = mine == 0
             return jnp.stack([jnp.where(first, near, far), jnp.where(first, far, near)])
 
-        rank = jnp.argsort(order)
-        ids = jnp.arange(num_experts)
-        position = rank - jnp.sum(jnp.where(expert_ids[:, None] == ids[None, :], starts[None, :], 0), axis=1)
-        place = jnp.where(lax.rem(expert_ids, 2) == mine, half, 0) + expert_ids // 2
-        token_slot = jnp.where(position < capacity, place * capacity + position, num_experts * capacity)
-
-        y_tok = take_rows([y_back], token_slot)[0].astype(F32)
+        y_rows = take_rows([y_back], token_slot)[0]
+        y_tok = y_rows.astype(F32)
         out_tokens = (gate_prob[:, None] * y_tok).astype(BF16)
         d_gate = jnp.sum(dy_f32 * y_tok, axis=-1)
         d_router_part, dx_router = router_backward(x_loc, router, log_probs, router_probs, expert_onehot, mod_mask, mean_probs, mod_count, d_gate)
-        dx_router = lax.optimization_barrier(dx_router)
-        dx_tokens = take_rows(dx_back, token_slot)[0] + dx_router
+        dx_tokens = take_rows(dx_back, token_slot, addend=dx_router)[0]
         dx_tokens, d_router_part = lax.optimization_barrier((dx_tokens, d_router_part))
-        d_router = device_sum(d_router_part.T.reshape(-1, 128), mesh, 2).reshape(num_experts, width).T
+        flat = d_router_part.T.reshape(-1, 128)
+        blocks = jnp.pad(flat, ((0, mesh.size * 8 - flat.shape[0]), (0, 0))).reshape(mesh.size, 8, 128)
+        d_router = device_sum(blocks, mesh, 2).reshape(-1, 128)[:flat.shape[0]].reshape(num_experts, width).T
         d_router, far_in1, far_out1, far_bias = lax.optimization_barrier((d_router, far_in1, far_out1, far_bias))
         d_w_in, d_w_out = join_grads((g_in0, g_in1), (far_in0, far_in1), (g_out0, g_out1), (far_out0, far_out1))
         bias = both(g_bias[0], far_bias[0])

time: 719 us -> 744 us (1.035)
  waiting for transfers between devices: 14.1 us -> 51.9 us
  starting transfers between devices: 15.5 us -> 49.3 us
  matrix products: 44.4 us -> 22.7 us
  other arithmetic: 65.4 us -> 53 us
  Pallas kernels: 560 us -> 550 us
    all_to_all x2, waiting for transfers between devices: 14.1 us -> 51.9 us  [swap_rows(): return lax.all_to_all(rows, 'ep', 0, 0, tiled=True)]
    all_to_all x2, starting transfers between devices: 11.9 us -> 46.6 us  [swap_rows(): return lax.all_to_all(rows, 'ep', 0, 0, tiled=True)]
    dot_general x3, matrix products: 43.3 us -> 21.6 us  [the longest x1 8.34 us: router_forward(): jnp.dot(x_loc, jnp.concatenate([high, mid, low], axis=1), preferred_eleme...]
    add x1, other arithmetic: 14.2 us -> 0.01 us  [router_backward(): pieces[:, 2 * num_experts:] + pieces[:, num_experts:2 * num_experts] + pi...]
    pallas_call x4 -> x5, Pallas kernels: 118 us -> 110 us  [take_rows(): pl.pallas_call(functools.partial(take_body, len(tables), n_outs, len(more...]
  transfers between devices with their start and end apart: 5 -> 5, of which waited for: 1 -> 1; matrix products, arithmetic and copies ran while one was open for 14% -> 7% of each run, Pallas kernels for 15% -> 11%
where the time goes in v3:
time: 744 us; the launch traced here: 742 us
  Pallas kernels  550 us (74%)
  other arithmetic  53 us (7%)
  waiting for transfers between devices  51.9 us (7%)
  starting transfers between devices  49.3 us (7%)
  matrix products  22.7 us (3%)
  local copies, waits for them, and re-layouts  11.3 us (2%)
    pallas_call x1, Pallas kernels, exchange_call(): pl.pallas_call(functools.partial(exchange_body, ep_size, count, fchunk),...  415 us
    pallas_call x5, Pallas kernels, take_rows(): pl.pallas_call(functools.partial(take_body, len(tables), n_outs, len(more...  110 us
    all_to_all x2, waiting for transfers between devices, swap_rows(): return lax.all_to_all(rows, 'ep', 0, 0, tiled=True)  51.9 us
    all_to_all x2, starting transfers between devices, swap_rows(): return lax.all_to_all(rows, 'ep', 0, 0, tiled=True)  46.6 us
    reduce_sum x1, other arithmetic, local_step(): d_gate = jnp.sum(dy_f32 * y_tok, axis=-1)  17.5 us
  transfers between devices with their start and end apart: 5, of which 1 were waited for; matrix products, arithmetic and copies ran while one was open for 7% of the time, Pallas kernels for 11%

profile of v3, /device:TPU:0, one launch (start us, length us, event | category | flops | bytes accessed | tf_op | source)
XLA Modules:
  0.0 741.7 jit_solution(4352294606314919356)
XLA Ops:
  0.6 0.9 convert_reduce_fusion
  2.4 0.8 multiply_add_fusion
  3.2 6.8 sort.31
  10.6 1.6 slots.1
  12.2 1.3 fusion.41.q_ref
  13.5 16.8 %take_rows.5 = bf16[4096,768]{1,0:T(8,128)(2,1)} custom-call(s32[4096]{0:T(1024)} %fusion.41.q_ref, bf16[8192,768]{1,0:T(8,128)(2,1)} %refs_0_.3), custom_call_target="tpu_custom_call" | custom-call | flops 134217728 | bytes 18874368 | tf_op jit(solution)/shard_map/take_rows/pallas_call | solution.py:213
  30.4 5.6 all-to-all-start
  36.1 8.3 %fusion.15 = f32[8192,48]{0,1:T(8,128)S(1)} fusion(bf16[8192,768]{1,0:T(8,128)(2,1)} %refs_0_.3, bf16[768,16]{0,1:T(8,128)(2,1)S(1)} %get-tuple-element.73, bf16[768,16]{0,1:T(8,128)(2,1)S(1)} %get-tuple-element.75, bf16[768,16]{0,1:T(8,128)(2,1)S(1)} %get-tuple-element.77), kind=kOutput, calls=%fused_computation.38 | convolution fusion | flops 604200960 | bytes 14229504 | tf_op jit(solution)/shard_map/dot_general | solution.py:613
  46.1 6.8 sort.32
  54.0 0.7 select_maximum_fusion.st_ref
  55.6 17.0 %take_rows.7 = bf16[4096,768]{1,0:T(8,128)(2,1)} custom-call(s32[4096]{0:T(1024)} %fusion.43.q_ref, bf16[8192,768]{1,0:T(8,128)(2,1)} %refs_0_.3), custom_call_target="tpu_custom_call" | custom-call | flops 134217728 | bytes 18874368 | tf_op jit(solution)/shard_map/take_rows/pallas_call | solution.py:213
  73.3 11.7 %fusion.refs_0_ = bf16[8192,768]{1,0:T(8,128)(2,1)} fusion(bf16[8192,768]{1,0:T(8,128)(2,1)} %param.19, f32[8192]{0:T(1024)S(1)} %get-tuple-element.68), kind=kLoop, calls=%fused_computation.3 | loop fusion | flops 18874368 | bytes 25198592 | tf_op jit(solution)/shard_map/convert_element_type | solution.py:676
  84.9 25.5 %take_rows.6 = (bf16[4096,768]{1,0:T(8,128)(2,1)}, bf16[4096,768]{1,0:T(8,128)(2,1)}) custom-call(s32[8192]{0:T(1024)} %fusion.29.q_ref, bf16[8192,768]{1,0:T(8,128)(2,1)} %fusion.refs_0_), custom_call_target="tpu_custom_call" | custom-call | flops 268435456 | bytes 25165824 | tf_op jit(solution)/shard_map/take_rows/pallas_call | solution.py:213
  110.4 0.7 fusion.27.q_ref
  111.1 414.9 %exchange.1 = (bf16[16,512,768]{2,1,0:T(8,128)(2,1)}, bf16[8,512,768]{2,1,0:T(8,128)(2,1)}, bf16[8,512,768]{2,1,0:T(8,128)(2,1)}, bf16[768,1536]{1,0:T(8,128)(2,...) custom-call(bf16[8,512,768]{2,1,0:T(8,128)(2,1)} %all-to-all-done.xo, ...), custom_call_target="tpu_custom_call" | custom-call | flops 270582939648 | bytes 75497472 | tf_op jit(solution)/shard_map/exchange/pallas_call | solution.py:591
  526.0 24.5 %take_rows.8 = bf16[8192,768]{1,0:T(8,128)(2,1)} custom-call(s32[8192]{0:T(1024)} %fusion.27.q_ref, bf16[8192,768]{1,0:T(8,128)(2,1)} %bitcast.80), custom_call_target="tpu_custom_call" | custom-call | flops 268435456 | bytes 25165824 | tf_op jit(solution)/shard_map/take_rows/pallas_call | solution.py:213
  550.5 17.5 %fusion.2 = (f32[8192]{0:T(1024)S(1)}, bf16[8192,768]{1,0:T(8,128)(2,1)}) fusion(bf16[8192,768]{1,0:T(8,128)(2,1)} %take_rows.8, bf16[8192,768]{1,0:T(8,128)(2,1)} %param.19, f32[8192]{0:T(1024)S(1)} %copy-done.12), kind=kLoop, calls=%fused_computation.5 | loop fusion | flops 37740544 | bytes 37814272 | tf_op jit(solution)/shard_map/reduce_sum | solution.py:704
  568.2 41.0 %all-to-all-start.1 = ((bf16[8,512,768]{2,1,0:T(8,128)(2,1)}), bf16[8,512,768]{2,1,0:T(8,128)(2,1)}, u32[]{:S(2)}, u32[]{:S(2)}) async-start(bf16[8,512,768]{2,1,0:T(8,128)(2,1)} %get-tuple-element.51), calls=%async_computation.1 | async-start | bytes 12582912 | tf_op jit(solution)/shard_map/all_to_all | solution.py:668
  609.3 0.7 collective-permute-start.2
  610.1 1.4 collective-permute-start
  613.7 0.7 fusion.54
  615.7 6.8 convolution_bitcast_fusion
  622.5 6.4 convolution_convert_fusion.refs_2_
  629.0 51.9 %all-to-all-done.1 = bf16[8,512,768]{2,1,0:T(8,128)(2,1)} async-done(((bf16[8,512,768]{2,1,0:T(8,128)(2,1)}), bf16[8,512,768]{2,1,0:T(8,128)(2,1)}, u32[]{:S(2)}, u32[]{:S(2)}) %all-to-all-start.1) | async-done | bytes 6291488 | tf_op jit(solution)/shard_map/all_to_all | solution.py:668
  680.9 26.7 %take_rows.9 = bf16[8192,768]{1,0:T(8,128)(2,1)} custom-call(s32[8192]{0:T(1024)} %fusion.27.q_ref, bf16[4096,768]{1,0:T(8,128)(2,1)} %bitcast.82, bf16[4096,768]{1,0:T(8,128)(2,1)} %bitcast.17.refs_1_, bf16[8192,768]{1,0:T(8,128)(2,1)} %convolution_convert_fusion.refs_2_), custom_call_target="tpu_custom_call" | custom-call | flops 268435456 | bytes 25165824 | tf_op jit(solution)/shard_map/take_rows/pallas_call | solution.py:213
  708.2 13.3 %device_sum.1 = f32[16,8,128]{2,1,0:T(8,128)} custom-call(f32[16,8,128]{2,1,0:T(8,128)} %pad_bitcast_fusion.x_ref), custom_call_target="tpu_custom_call" | custom-call | flops 10000000 | bytes 1000000 | tf_op jit(solution)/shard_map/device_sum/pallas_call | solution.py:102
  721.5 0.8 slice.66
  724.2 1.7 copy-done
  725.9 1.7 copy-done.1
  727.5 1.7 copy-done.2
  729.2 1.7 copy-done.3
  730.9 9.7 %join_grads.1 = (bf16[2,768,3072]{2,1,0:T(8,128)(2,1)}, bf16[2,3072,768]{2,1,0:T(8,128)(2,1)}) custom-call(bf16[768,1536]{1,0:T(8,128)(2,1)S(1)} %copy-done, bf16[768,1536]{1,0:T(8,128)(2,1)S(1)} %copy-done.2, bf16[768,1536]{1,0:T(8,128)(2,1)} %get-tuple-element.54.refs_2_, bf16[768,1536]{1,0:T(8,128)(2,1)} %collective-permute-done.refs_3_, ...), custom_call_target="tpu_custom_call" | custom-call | flops 10000000 | bytes 37748736 | tf_op jit(solution)/shard_map/join_grads/pallas_call | solution.py:252
  (108 shorter events, 10.8 us)
Async XLA Ops:
  30.4 5.6 copy-start.10
  30.4 80.7 %all-to-all-start = ((bf16[8,512,768]{2,1,0:T(8,128)(2,1)}), bf16[8,512,768]{2,1,0:T(8,128)(2,1)}, u32[]{:S(2)}, u32[]{:S(2)}) async-start(bf16[8,512,768]{2,1,0:T(8,128)(2,1)} %bitcast.79), calls=%async_computation | async-start | bytes 12582912 | tf_op jit(solution)/shard_map/all_to_all | solution.py:668
  36.0 8.4 %copy-start.25 = (bf16[2,768]{1,0:T(2,128)(2,1)S(1)}, bf16[2,768]{1,0:T(2,128)(2,1)}, u32[]{:S(2)}) copy-start(bf16[2,768]{1,0:T(2,128)(2,1)} %param.18) | copy-start | bytes 9220
  36.0 9.0 %copy-start.19 = (s32[8192]{0:T(1024)S(1)}, s32[8192]{0:T(1024)}, u32[]{:S(2)}) copy-start(s32[8192]{0:T(1024)} %param.11) | copy-start | bytes 98308
  36.0 9.1 %copy-start.23 = (bf16[2,3072]{1,0:T(2,128)(2,1)S(1)}, bf16[2,3072]{1,0:T(2,128)(2,1)}, u32[]{:S(2)}) copy-start(bf16[2,3072]{1,0:T(2,128)(2,1)} %param.16) | copy-start | bytes 36868
  36.1 17.1 %copy-start.6 = (s32[8192]{0:T(1024)S(1)}, s32[8192]{0:T(1024)}, u32[]{:S(2)}) copy-start(s32[8192]{0:T(1024)} %param.13) | copy-start | bytes 98308
  36.1 17.4 %copy-start.21 = (s32[64,128]{1,0:T(8,128)S(1)}, s32[64,128]{1,0:T(8,128)}, u32[]{:S(2)}) copy-start(s32[64,128]{1,0:T(8,128)} %get-tuple-element.39) | copy-start | bytes 98308
  46.0 8.9 %copy-start.17 = (pred[2,8192]{1,0:T(4,128)(4,1)}, pred[2,8192]{1,0:T(4,128)(4,1)S(1)}, u32[]{:S(2)}) copy-start(pred[2,8192]{1,0:T(4,128)(4,1)S(1)} %get-tuple-element.88) | copy-start | bytes 49156
  53.0 0.8 copy-start.4
  53.0 1.9 copy-start.8
  53.2 1.8 copy-start.13
  53.5 19.8 %copy-start.11 = (f32[8192]{0:T(1024)}, f32[8192]{0:T(1024)S(1)}, u32[]{:S(2)}) copy-start(f32[8192]{0:T(1024)S(1)} %get-tuple-element.68) | copy-start | bytes 98308
  55.6 17.0 %copy-start.20 = (s32[64,128]{1,0:T(8,128)S(1)}, s32[64,128]{1,0:T(8,128)}, u32[]{:S(2)}) copy-start(s32[64,128]{1,0:T(8,128)} %get-tuple-element.43) | copy-start | bytes 98308
  110.4 415.5 %copy-start.15 = (bf16[768,96]{0,1:T(8,128)(2,1)}, bf16[768,96]{0,1:T(8,128)(2,1)S(1)}, u32[]{:S(2)}) copy-start(bf16[768,96]{0,1:T(8,128)(2,1)S(1)} %constant_dynamic-update-slice_fusion.6) | copy-start | bytes 442372
  525.9 24.5 %copy-start.12 = (f32[8192]{0:T(1024)S(1)}, f32[8192]{0:T(1024)}, u32[]{:S(2)}) copy-start(f32[8192]{0:T(1024)} %copy-done.11) | copy-start | bytes 98308
  550.4 17.5 %copy-start.26 = (f32[8,128]{1,0:T(8,128)S(1)}, f32[8,128]{1,0:T(8,128)}, u32[]{:S(2)}) copy-start(f32[8,128]{1,0:T(8,128)} %get-tuple-element.49) | copy-start | bytes 12292
  550.4 17.7 %copy-start.24 = (f32[1,768]{1,0:T(1,128)S(1)}, f32[1,768]{1,0:T(1,128)}, u32[]{:S(2)}) copy-start(f32[1,768]{1,0:T(1,128)} %get-tuple-element.57) | copy-start | bytes 9220
  568.2 41.0 %copy-start.22 = (f32[1,3072]{1,0:T(1,128)S(1)}, f32[1,3072]{1,0:T(1,128)}, u32[]{:S(2)}) copy-start(f32[1,3072]{1,0:T(1,128)} %get-tuple-element.56) | copy-start | bytes 36868
  568.2 41.8 %copy-start.18 = (pred[2,8192]{1,0:T(4,128)(4,1)S(1)}, pred[2,8192]{1,0:T(4,128)(4,1)}, u32[]{:S(2)}) copy-start(pred[2,8192]{1,0:T(4,128)(4,1)} %copy-done.17) | copy-start | bytes 49156
  568.2 44.0 %copy-start.5 = (f32[8192,16]{0,1:T(8,128)S(1)}, f32[8192,16]{0,1:T(8,128)}, u32[]{:S(2)}) copy-start(f32[8192,16]{0,1:T(8,128)} %copy-done.4) | copy-start | bytes 1572868
  568.2 44.0 %copy-start.7 = (s32[8192]{0:T(1024)S(1)}, s32[8192]{0:T(1024)}, u32[]{:S(2)}) copy-start(s32[8192]{0:T(1024)} %param.13) | copy-start | bytes 98308
  568.2 44.0 %copy-start.9 = (f32[8192]{0:T(1024)S(1)}, f32[8192]{0:T(1024)}, u32[]{:S(2)}) copy-start(f32[8192]{0:T(1024)} %copy-done.8) | copy-start | bytes 98308
  568.2 44.0 %copy-start.14 = (f32[8192]{0:T(1024)S(1)}, f32[8192]{0:T(1024)}, u32[]{:S(2)}) copy-start(f32[8192]{0:T(1024)} %copy-done.13) | copy-start | bytes 98308
  568.2 112.6 %all-to-all-start.1 = ((bf16[8,512,768]{2,1,0:T(8,128)(2,1)}), bf16[8,512,768]{2,1,0:T(8,128)(2,1)}, u32[]{:S(2)}, u32[]{:S(2)}) async-start(bf16[8,512,768]{2,1,0:T(8,128)(2,1)} %get-tuple-element.51), calls=%async_computation.1 | async-start | bytes 12582912 | tf_op jit(solution)/shard_map/all_to_all | solution.py:668
  609.3 113.6 %collective-permute-start.2 = (bf16[1,3840]{1,0:T(2,128)(2,1)S(1)}, bf16[1,3840]{1,0:T(2,128)(2,1)S(1)}, u32[]{:S(2)}, u32[]{:S(2)}) collective-permute-start(bf16[1,3840]{1,0:T(2,128)(2,1)S(1)} %pad_maximum_fusion), channel_id=1, source_target_pairs={{0,8},{8,0},{1,9},{9,1},{2,10},{10,2},{3,11},{11,3},{4,12},{12,4},... | collective-permute-start | bytes 23048 | tf_op jit(solution)/shard_map/ppermute | solution.py:695
  610.1 112.8 %collective-permute-start = (bf16[768,1536]{1,0:T(8,128)(2,1)}, bf16[768,1536]{1,0:T(8,128)(2,1)}, u32[]{:S(2)}, u32[]{:S(2)}) collective-permute-start(bf16[768,1536]{1,0:T(8,128)(2,1)} %get-tuple-element.54.refs_2_), channel_id=1, source_target_pairs={{0,8},{8,0},{1,9},{9,1},{2,10},{10,2},{3,11},{11,3},{4,12},{12,4},... | collective-permute-start | bytes 7077896 | tf_op jit(solution)/shard_map/ppermute | solution.py:694
  611.5 111.4 %collective-permute-start.1 = (bf16[1536,768]{1,0:T(8,128)(2,1)}, bf16[1536,768]{1,0:T(8,128)(2,1)}, u32[]{:S(2)}, u32[]{:S(2)}) collective-permute-start(bf16[1536,768]{1,0:T(8,128)(2,1)} %get-tuple-element.55.refs_6_), channel_id=1, source_target_pairs={{0,8},{8,0},{1,9},{9,1},{2,10},{10,2},{3,11},{11,3},{4,12},{12,4},... | collective-permute-start | bytes 7077896 | tf_op jit(solution)/shard_map/ppermute | solution.py:693
  615.7 6.9 copy-start.16
  724.2 1.7 copy-start
  725.9 1.7 copy-start.1
  727.5 1.7 copy-start.2
  729.2 1.7 copy-start.3

commit v4 on v3

--- a/solution.py
+++ b/solution.py
@@ -225,17 +225,16 @@
     )(q, *tables, *more)
 
 
-def join_body(*refs):
-    pieces, outs, bufs, sems = refs[:8], refs[8:10], refs[10:12], refs[12:]
+def join_body(places, count, *refs):
+    pieces, outs, (bufs, sem_in, sem_out) = refs[:len(places)], refs[count:count + 2], refs[count + 2:]
     mine = lax.axis_index("dp")
     copies = []
-    for i, src in enumerate(pieces):
-        kind, part, far = i // 4, (i // 2) % 2, i % 2
+    for i, (src, (kind, part, far)) in enumerate(zip(pieces, places)):
         owner = 1 - mine if far else mine
         rows, cols = src.shape
         dst = outs[0].at[owner, :, pl.ds(part * cols, cols)] if kind == 0 else outs[1].at[owner, pl.ds(part * rows, rows), :]
-        buf = bufs[kind].at[i % 4]
-        copies.append((pltpu.make_async_copy(src, buf, sems[0].at[i]), pltpu.make_async_copy(buf, dst, sems[1].at[i])))
+        buf = bufs.at[i, pl.ds(0, rows), pl.ds(0, cols)]
+        copies.append((pltpu.make_async_copy(src, buf, sem_in.at[i]), pltpu.make_async_copy(buf, dst, sem_out.at[i])))
     for c in copies:
         c[0].start()
     for c in copies:
@@ -245,21 +244,24 @@
         c[1].wait()
 
 
-def join_grads(near1, far1, near2, far2):
-    width, part = near1[0].shape
+def join_grads(pieces, places, width, hidden, into=None):
     anyspec = pl.BlockSpec(memory_space=pl.ANY)
-    pieces = [near1[0], far1[0], near1[1], far1[1], near2[0], far2[0], near2[1], far2[1]]
+    held = [] if into is None else list(into)
+    count = len(pieces) + len(held)
+    part = hidden // 2
+    side = max(width, part)
     return pl.pallas_call(
-        join_body,
-        in_specs=[anyspec] * 8,
+        functools.partial(join_body, places, count),
+        in_specs=[anyspec] * count,
         out_specs=[anyspec] * 2,
-        out_shape=[jax.ShapeDtypeStruct((2, width, 2 * part), BF16), jax.ShapeDtypeStruct((2, 2 * part, width), BF16)],
-        scratch_shapes=[pltpu.VMEM((4, width, part), BF16), pltpu.VMEM((4, part, width), BF16),
-                        pltpu.SemaphoreType.DMA((8,)), pltpu.SemaphoreType.DMA((8,))],
-        compiler_params=pltpu.CompilerParams(vmem_limit_bytes=40_000_000),
-        cost_estimate=pl.CostEstimate(flops=10_000_000, bytes_accessed=16 * width * part * 2, transcendentals=0),
+        out_shape=[jax.ShapeDtypeStruct((2, width, hidden), BF16), jax.ShapeDtypeStruct((2, hidden, width), BF16)],
+        input_output_aliases={len(pieces) + i: i for i in range(len(held))},
+        scratch_shapes=[pltpu.VMEM((len(pieces), side, side), BF16),
+                        pltpu.SemaphoreType.DMA((len(pieces),)), pltpu.SemaphoreType.DMA((len(pieces),))],
+        compiler_params=pltpu.CompilerParams(vmem_limit_bytes=VMEM_CAP),
+        cost_estimate=pl.CostEstimate(flops=10_000_000, bytes_accessed=4 * len(pieces) * width * part, transcendentals=0),
         name="join_grads",
-    )(*pieces)
+    )(*pieces, *held)
 
 
 def exchange_body(ep_size, count, fchunk,
@@ -700,6 +702,8 @@
 
         y_rows = take_rows([y_back], token_slot)[0]
         y_tok = y_rows.astype(F32)
+        joined = join_grads([g_in0, far_in0, g_in1, g_out0, far_out0, g_out1],
+                            ((0, 0, False), (0, 0, True), (0, 1, False), (1, 0, False), (1, 0, True), (1, 1, False)), width, w_in.shape[-1])
         out_tokens = (gate_prob[:, None] * y_tok).astype(BF16)
         d_gate = jnp.sum(dy_f32 * y_tok, axis=-1)
         d_router_part, dx_router = router_backward(x_loc, router, log_probs, router_probs, expert_onehot, mod_mask, mean_probs, mod_count, d_gate)
@@ -709,7 +713,8 @@
         blocks = jnp.pad(flat, ((0, mesh.size * 8 - flat.shape[0]), (0, 0))).reshape(mesh.size, 8, 128)
         d_router = device_sum(blocks, mesh, 2).reshape(-1, 128)[:flat.shape[0]].reshape(num_experts, width).T
         d_router, far_in1, far_out1, far_bias = lax.optimization_barrier((d_router, far_in1, far_out1, far_bias))
-        d_w_in, d_w_out = join_grads((g_in0, g_in1), (far_in0, far_in1), (g_out0, g_out1), (far_out0, far_out1))
+        hidden = w_in.shape[-1]
+        d_w_in, d_w_out = join_grads([far_in1, far_out1], ((0, 1, True), (1, 1, True)), width, hidden, into=joined)
         bias = both(g_bias[0], far_bias[0])
         hidden = w_in.shape[-1]
         return (out_tokens, aux_loss, dx_tokens, d_router, d_w_in, bias[:, :hidden], d_w_out, bias[:, hidden:])

time: 744 us -> 731 us (0.983)
  waiting for transfers between devices: 51.9 us -> 40.6 us
    all_to_all x2, waiting for transfers between devices: 51.9 us -> 40.6 us  [swap_rows(): return lax.all_to_all(rows, 'ep', 0, 0, tiled=True)]
  transfers between devices with their start and end apart: 5 -> 5, of which waited for: 1 -> 1; matrix products, arithmetic and copies ran while one was open for 7% -> 7% of each run, Pallas kernels for 11% -> 13%
where the time goes in v4:
time: 731 us; the launch traced here: 729 us
  Pallas kernels  554 us (76%)
  other arithmetic  53 us (7%)
  starting transfers between devices  49.3 us (7%)
  waiting for transfers between devices  40.6 us (6%)
  matrix products  22.8 us (3%)
    pallas_call x1, Pallas kernels, exchange_call(): pl.pallas_call(functools.partial(exchange_body, ep_size, count, fchunk),...  415 us
    pallas_call x5, Pallas kernels, take_rows(): pl.pallas_call(functools.partial(take_body, len(tables), n_outs, len(more...  110 us
    all_to_all x2, starting transfers between devices, swap_rows(): return lax.all_to_all(rows, 'ep', 0, 0, tiled=True)  46.6 us
    all_to_all x2, waiting for transfers between devices, swap_rows(): return lax.all_to_all(rows, 'ep', 0, 0, tiled=True)  40.6 us
    reduce_sum x1, other arithmetic, local_step(): d_gate = jnp.sum(dy_f32 * y_tok, axis=-1)  17.5 us
  transfers between devices with their start and end apart: 5, of which 1 were waited for; matrix products, arithmetic and copies ran while one was open for 7% of the time, Pallas kernels for 13%

profile of v4, /device:TPU:0, one launch (start us, length us, event | category | flops | bytes accessed | tf_op | source)
XLA Modules:
  0.0 729.2 jit_solution(13712271080703226517)
XLA Ops:
  0.6 0.9 convert_reduce_fusion
  2.4 0.8 multiply_add_fusion
  3.2 6.8 sort.31
  10.6 1.6 slots.1
  12.2 1.3 fusion.41.q_ref
  13.5 16.8 %take_rows.5 = bf16[4096,768]{1,0:T(8,128)(2,1)} custom-call(s32[4096]{0:T(1024)} %fusion.41.q_ref, bf16[8192,768]{1,0:T(8,128)(2,1)} %refs_0_.3), custom_call_target="tpu_custom_call" | custom-call | flops 134217728 | bytes 18874368 | tf_op jit(solution)/shard_map/take_rows/pallas_call | solution.py:213
  30.4 5.6 all-to-all-start
  36.1 8.3 %fusion.15 = f32[8192,48]{0,1:T(8,128)S(1)} fusion(bf16[8192,768]{1,0:T(8,128)(2,1)} %refs_0_.3, bf16[768,16]{0,1:T(8,128)(2,1)S(1)} %get-tuple-element.77, bf16[768,16]{0,1:T(8,128)(2,1)S(1)} %get-tuple-element.79, bf16[768,16]{0,1:T(8,128)(2,1)S(1)} %get-tuple-element.81), kind=kOutput, calls=%fused_computation.38 | convolution fusion | flops 604200960 | bytes 14229504 | tf_op jit(solution)/shard_map/dot_general | solution.py:615
  46.1 6.8 sort.32
  54.0 0.7 select_maximum_fusion.st_ref
  55.6 17.0 %take_rows.7 = bf16[4096,768]{1,0:T(8,128)(2,1)} custom-call(s32[4096]{0:T(1024)} %fusion.43.q_ref, bf16[8192,768]{1,0:T(8,128)(2,1)} %refs_0_.3), custom_call_target="tpu_custom_call" | custom-call | flops 134217728 | bytes 18874368 | tf_op jit(solution)/shard_map/take_rows/pallas_call | solution.py:213
  72.6 0.7 fusion.29.q_ref
  73.3 11.7 %fusion.refs_0_ = bf16[8192,768]{1,0:T(8,128)(2,1)} fusion(bf16[8192,768]{1,0:T(8,128)(2,1)} %param.19, f32[8192]{0:T(1024)S(1)} %get-tuple-element.72), kind=kLoop, calls=%fused_computation.3 | loop fusion | flops 18874368 | bytes 25198592 | tf_op jit(solution)/shard_map/convert_element_type | solution.py:678
  84.9 25.5 %take_rows.6 = (bf16[4096,768]{1,0:T(8,128)(2,1)}, bf16[4096,768]{1,0:T(8,128)(2,1)}) custom-call(s32[8192]{0:T(1024)} %fusion.29.q_ref, bf16[8192,768]{1,0:T(8,128)(2,1)} %fusion.refs_0_), custom_call_target="tpu_custom_call" | custom-call | flops 268435456 | bytes 25165824 | tf_op jit(solution)/shard_map/take_rows/pallas_call | solution.py:213
  110.4 0.7 fusion.27.q_ref
  111.1 414.9 %exchange.1 = (bf16[16,512,768]{2,1,0:T(8,128)(2,1)}, bf16[8,512,768]{2,1,0:T(8,128)(2,1)}, bf16[8,512,768]{2,1,0:T(8,128)(2,1)}, bf16[768,1536]{1,0:T(8,128)(2,...) custom-call(bf16[8,512,768]{2,1,0:T(8,128)(2,1)} %all-to-all-done.xo, ...), custom_call_target="tpu_custom_call" | custom-call | flops 270582939648 | bytes 75497472 | tf_op jit(solution)/shard_map/exchange/pallas_call | solution.py:593
  526.0 24.5 %take_rows.8 = bf16[8192,768]{1,0:T(8,128)(2,1)} custom-call(s32[8192]{0:T(1024)} %fusion.27.q_ref, bf16[8192,768]{1,0:T(8,128)(2,1)} %bitcast.80), custom_call_target="tpu_custom_call" | custom-call | flops 268435456 | bytes 25165824 | tf_op jit(solution)/shard_map/take_rows/pallas_call | solution.py:213
  550.5 17.5 %fusion.2 = (f32[8192]{0:T(1024)S(1)}, bf16[8192,768]{1,0:T(8,128)(2,1)}) fusion(bf16[8192,768]{1,0:T(8,128)(2,1)} %take_rows.8, bf16[8192,768]{1,0:T(8,128)(2,1)} %param.19, f32[8192]{0:T(1024)S(1)} %copy-done.10), kind=kLoop, calls=%fused_computation.5 | loop fusion | flops 37740544 | bytes 37814272 | tf_op jit(solution)/shard_map/reduce_sum | solution.py:708
  568.2 41.0 %all-to-all-start.1 = ((bf16[8,512,768]{2,1,0:T(8,128)(2,1)}), bf16[8,512,768]{2,1,0:T(8,128)(2,1)}, u32[]{:S(2)}, u32[]{:S(2)}) async-start(bf16[8,512,768]{2,1,0:T(8,128)(2,1)} %get-tuple-element.53), calls=%async_computation.1 | async-start | bytes 12582912 | tf_op jit(solution)/shard_map/all_to_all | solution.py:670
  609.3 0.7 collective-permute-start.2
  610.1 1.4 collective-permute-start
  611.5 0.6 collective-permute-start.1
  613.1 1.1 copy-done.2
  614.8 0.7 fusion.54
  616.8 10.0 %join_grads.2 = (bf16[2,768,3072]{2,1,0:T(8,128)(2,1)}, bf16[2,3072,768]{2,1,0:T(8,128)(2,1)}) custom-call(bf16[768,1536]{1,0:T(8,128)(2,1)} %get-tuple-element.63.refs_0_, bf16[768,1536]{1,0:T(8,128)(2,1)} %get-tuple-element.64.refs_1_, bf16[768,1536]{1,0:T(8,128)(2,1)} %get-tuple-element.56.refs_2_, bf16[1536,768]{1,0:T(8,128)(2,1)} %get-tuple-element.65.refs_3_, ...), custom_call_target="tpu_custom_call" | custom-call | flops 10000000 | bytes 28311552 | tf_op jit(solution)/shard_map/join_grads/pallas_call | solution.py:253
  626.9 6.9 convolution_bitcast_fusion
  633.8 6.4 convolution_convert_fusion.refs_2_
  640.3 40.6 %all-to-all-done.1 = bf16[8,512,768]{2,1,0:T(8,128)(2,1)} async-done(((bf16[8,512,768]{2,1,0:T(8,128)(2,1)}), bf16[8,512,768]{2,1,0:T(8,128)(2,1)}, u32[]{:S(2)}, u32[]{:S(2)}) %all-to-all-start.1) | async-done | bytes 6291488 | tf_op jit(solution)/shard_map/all_to_all | solution.py:670
  680.9 26.7 %take_rows.9 = bf16[8192,768]{1,0:T(8,128)(2,1)} custom-call(s32[8192]{0:T(1024)} %fusion.27.q_ref, bf16[4096,768]{1,0:T(8,128)(2,1)} %bitcast.82, bf16[4096,768]{1,0:T(8,128)(2,1)} %bitcast.17.refs_1_, bf16[8192,768]{1,0:T(8,128)(2,1)} %convolution_convert_fusion.refs_2_), custom_call_target="tpu_custom_call" | custom-call | flops 268435456 | bytes 25165824 | tf_op jit(solution)/shard_map/take_rows/pallas_call | solution.py:213
  708.2 13.3 %device_sum.1 = f32[16,8,128]{2,1,0:T(8,128)} custom-call(f32[16,8,128]{2,1,0:T(8,128)} %pad_bitcast_fusion.x_ref), custom_call_target="tpu_custom_call" | custom-call | flops 10000000 | bytes 1000000 | tf_op jit(solution)/shard_map/device_sum/pallas_call | solution.py:102
  721.5 0.8 slice.66
  724.2 3.9 join_grads.3
  (105 shorter events, 9.5 us)
Async XLA Ops:
  30.4 5.6 copy-start.8
  30.4 80.7 %all-to-all-start = ((bf16[8,512,768]{2,1,0:T(8,128)(2,1)}), bf16[8,512,768]{2,1,0:T(8,128)(2,1)}, u32[]{:S(2)}, u32[]{:S(2)}) async-start(bf16[8,512,768]{2,1,0:T(8,128)(2,1)} %bitcast.79), calls=%async_computation | async-start | bytes 12582912 | tf_op jit(solution)/shard_map/all_to_all | solution.py:670
  36.0 8.4 %copy-start.23 = (bf16[2,768]{1,0:T(2,128)(2,1)S(1)}, bf16[2,768]{1,0:T(2,128)(2,1)}, u32[]{:S(2)}) copy-start(bf16[2,768]{1,0:T(2,128)(2,1)} %param.18) | copy-start | bytes 9220
  36.0 9.0 %copy-start.17 = (s32[8192]{0:T(1024)S(1)}, s32[8192]{0:T(1024)}, u32[]{:S(2)}) copy-start(s32[8192]{0:T(1024)} %param.11) | copy-start | bytes 98308
  36.0 9.1 %copy-start.21 = (bf16[2,3072]{1,0:T(2,128)(2,1)S(1)}, bf16[2,3072]{1,0:T(2,128)(2,1)}, u32[]{:S(2)}) copy-start(bf16[2,3072]{1,0:T(2,128)(2,1)} %param.16) | copy-start | bytes 36868
  36.1 17.1 %copy-start.4 = (s32[8192]{0:T(1024)S(1)}, s32[8192]{0:T(1024)}, u32[]{:S(2)}) copy-start(s32[8192]{0:T(1024)} %param.13) | copy-start | bytes 98308
  36.1 17.4 %copy-start.19 = (s32[64,128]{1,0:T(8,128)S(1)}, s32[64,128]{1,0:T(8,128)}, u32[]{:S(2)}) copy-start(s32[64,128]{1,0:T(8,128)} %get-tuple-element.41) | copy-start | bytes 98308
  46.0 8.9 %copy-start.15 = (pred[2,8192]{1,0:T(4,128)(4,1)}, pred[2,8192]{1,0:T(4,128)(4,1)S(1)}, u32[]{:S(2)}) copy-start(pred[2,8192]{1,0:T(4,128)(4,1)S(1)} %get-tuple-element.92) | copy-start | bytes 49156
  53.0 0.8 copy-start
  53.0 1.9 copy-start.6
  53.2 1.8 copy-start.11
  53.5 19.8 %copy-start.9 = (f32[8192]{0:T(1024)}, f32[8192]{0:T(1024)S(1)}, u32[]{:S(2)}) copy-start(f32[8192]{0:T(1024)S(1)} %get-tuple-element.72) | copy-start | bytes 98308
  55.6 17.0 %copy-start.18 = (s32[64,128]{1,0:T(8,128)S(1)}, s32[64,128]{1,0:T(8,128)}, u32[]{:S(2)}) copy-start(s32[64,128]{1,0:T(8,128)} %get-tuple-element.45) | copy-start | bytes 98308
  110.4 415.5 %copy-start.13 = (bf16[768,96]{0,1:T(8,128)(2,1)}, bf16[768,96]{0,1:T(8,128)(2,1)S(1)}, u32[]{:S(2)}) copy-start(bf16[768,96]{0,1:T(8,128)(2,1)S(1)} %constant_dynamic-update-slice_fusion.6) | copy-start | bytes 442372
  525.9 24.5 %copy-start.10 = (f32[8192]{0:T(1024)S(1)}, f32[8192]{0:T(1024)}, u32[]{:S(2)}) copy-start(f32[8192]{0:T(1024)} %copy-done.9) | copy-start | bytes 98308
  550.4 17.5 %copy-start.24 = (f32[8,128]{1,0:T(8,128)S(1)}, f32[8,128]{1,0:T(8,128)}, u32[]{:S(2)}) copy-start(f32[8,128]{1,0:T(8,128)} %get-tuple-element.51) | copy-start | bytes 12292
  550.4 17.7 %copy-start.22 = (f32[1,768]{1,0:T(1,128)S(1)}, f32[1,768]{1,0:T(1,128)}, u32[]{:S(2)}) copy-start(f32[1,768]{1,0:T(1,128)} %get-tuple-element.59) | copy-start | bytes 9220
  568.2 41.1 %copy-start.20 = (f32[1,3072]{1,0:T(1,128)S(1)}, f32[1,3072]{1,0:T(1,128)}, u32[]{:S(2)}) copy-start(f32[1,3072]{1,0:T(1,128)} %get-tuple-element.58) | copy-start | bytes 36868
  568.2 41.8 %copy-start.16 = (pred[2,8192]{1,0:T(4,128)(4,1)S(1)}, pred[2,8192]{1,0:T(4,128)(4,1)}, u32[]{:S(2)}) copy-start(pred[2,8192]{1,0:T(4,128)(4,1)} %copy-done.15) | copy-start | bytes 49156
  568.2 44.0 %copy-start.1 = (f32[8192,16]{0,1:T(8,128)S(1)}, f32[8192,16]{0,1:T(8,128)}, u32[]{:S(2)}) copy-start(f32[8192,16]{0,1:T(8,128)} %copy-done) | copy-start | bytes 1572868
  568.2 44.0 %copy-start.5 = (s32[8192]{0:T(1024)S(1)}, s32[8192]{0:T(1024)}, u32[]{:S(2)}) copy-start(s32[8192]{0:T(1024)} %param.13) | copy-start | bytes 98308
  568.2 44.0 %copy-start.7 = (f32[8192]{0:T(1024)S(1)}, f32[8192]{0:T(1024)}, u32[]{:S(2)}) copy-start(f32[8192]{0:T(1024)} %copy-done.6) | copy-start | bytes 98308
  568.2 44.0 %copy-start.12 = (f32[8192]{0:T(1024)S(1)}, f32[8192]{0:T(1024)}, u32[]{:S(2)}) copy-start(f32[8192]{0:T(1024)} %copy-done.11) | copy-start | bytes 98308
  568.2 112.6 %all-to-all-start.1 = ((bf16[8,512,768]{2,1,0:T(8,128)(2,1)}), bf16[8,512,768]{2,1,0:T(8,128)(2,1)}, u32[]{:S(2)}, u32[]{:S(2)}) async-start(bf16[8,512,768]{2,1,0:T(8,128)(2,1)} %get-tuple-element.53), calls=%async_computation.1 | async-start | bytes 12582912 | tf_op jit(solution)/shard_map/all_to_all | solution.py:670
  609.3 113.6 %collective-permute-start.2 = (bf16[1,3840]{1,0:T(2,128)(2,1)S(1)}, bf16[1,3840]{1,0:T(2,128)(2,1)S(1)}, u32[]{:S(2)}, u32[]{:S(2)}) collective-permute-start(bf16[1,3840]{1,0:T(2,128)(2,1)S(1)} %pad_maximum_fusion), channel_id=1, source_target_pairs={{0,8},{8,0},{1,9},{9,1},{2,10},{10,2},{3,11},{11,3},{4,12},{12,4},... | collective-permute-start | bytes 23048 | tf_op jit(solution)/shard_map/ppermute | solution.py:697
  610.1 112.8 %collective-permute-start = (bf16[768,1536]{1,0:T(8,128)(2,1)}, bf16[768,1536]{1,0:T(8,128)(2,1)}, u32[]{:S(2)}, u32[]{:S(2)}) collective-permute-start(bf16[768,1536]{1,0:T(8,128)(2,1)} %get-tuple-element.56.refs_2_), channel_id=1, source_target_pairs={{0,8},{8,0},{1,9},{9,1},{2,10},{10,2},{3,11},{11,3},{4,12},{12,4},... | collective-permute-start | bytes 7077896 | tf_op jit(solution)/shard_map/ppermute | solution.py:696
  611.5 111.4 %collective-permute-start.1 = (bf16[1536,768]{1,0:T(8,128)(2,1)}, bf16[1536,768]{1,0:T(8,128)(2,1)}, u32[]{:S(2)}, u32[]{:S(2)}) collective-permute-start(bf16[1536,768]{1,0:T(8,128)(2,1)} %get-tuple-element.57.refs_5_), channel_id=1, source_target_pairs={{0,8},{8,0},{1,9},{9,1},{2,10},{10,2},{3,11},{11,3},{4,12},{12,4},... | collective-permute-start | bytes 7077896 | tf_op jit(solution)/shard_map/ppermute | solution.py:695
  613.1 1.1 copy-start.2
  626.8 7.0 copy-start.3
  626.8 7.0 copy-start.14
